TPU v7x, 32 devices: a whole 2x2x4 slice. The times are simulated.
32 devices in a mesh: node: 8 (over z, core), group: 4 (over y, x).
Axes of the slice: x: 2, y: 2, z: 4, core: 2. Of those that a mesh axis runs over, the one named last changes fastest.
Arguments:
- gradient: bfloat16 [8, 4, 128, 1024], P('node', 'group'), may hold values from -60 to 60
- momentum: float32 [128, 1024], replicated, may hold values from -6 to 6
- variance: float32 [128, 1024], replicated, may hold values from 0.004 to 0.4
- params: float32 [128, 1024], replicated, may hold values from -6 to 6
- worker_error: float32 [8, 4, 128, 1024], P('node', 'group'), may hold values from -18 to 18, as said below
- server_error: float32 [4, 128, 1024], P('group', 'node'), may hold values from -12 to 12, as said below
- group_worker_error: float32 [4, 128, 1024], P('group', 'node'), may hold values from -12 to 12, as said below
- group_server_error: float32 [128, 1024], P(('node', 'group')), may hold values from -12 to 12, as said below
Outputs:
- new_params: float32 [128, 1024], replicated
- new_momentum: float32 [128, 1024], replicated
- new_worker_error: float32 [8, 4, 128, 1024], P('node', 'group')
- new_server_error: float32 [4, 128, 1024], P('group', 'node')
- new_group_worker_error: float32 [4, 128, 1024], P('group', 'node')
- new_group_server_error: float32 [128, 1024], P(('node', 'group'))
Inputs may be any that keep to these rules, and one draw needn't show every extreme that they name: `worker_error`: no entry of local has magnitude under 0.005. No entry of group_mean + server_error has magnitude under 0.005. No entry of group_q + group_worker_error has magnitude under 0.005. No entry of total_mean + group_server_error has magnitude under 0.005.
All inputs are finite; a program needn't handle non-finite values.
Results may differ from a plain program's by a relative error of at most 0.0003.
Values sent between devices are 32-bit elements; how exact they have to be, the bound alone decides.
No kernel may reach another device: no remote copies, remote signals or barrier semaphores. Data moves between devices by JAX's collectives and lax.ppermute only.
A program may use at most 128 MiB of HBM per device.

v0:
```python
import jax
import jax.numpy as jnp
from jax import lax
from jax.sharding import PartitionSpec as P


def compress(values):
    scale = jnp.mean(jnp.abs(values), axis=-1, keepdims=True)
    packed = scale * jnp.sign(values)
    return (packed, values - packed)


def body(
    gradient,
    momentum,
    variance,
    params,
    worker_error,
    server_error,
    group_worker_error,
    group_server_error,
):
    nodes = lax.axis_size("node")
    groups = lax.axis_size("group")
    rows = momentum.shape[0]
    width = momentum.shape[1]
    shard_rows = rows // nodes
    local = 0.9 * momentum + 0.1 * gradient[0, 0].astype(jnp.float32) + worker_error[0, 0]
    first, new_worker_error = compress(local)
    arrived = lax.all_to_all(
        first.reshape(nodes, shard_rows, width), "node", split_axis=0, concat_axis=0, tiled=True
    )
    group_mean = jnp.sum(arrived, axis=0) / nodes
    group_q, new_server_error = compress(group_mean + server_error[0])
    second, new_group_worker_error = compress(group_q + group_worker_error[0])
    received = lax.all_to_all(
        second.reshape(groups, shard_rows // groups, width),
        "group",
        split_axis=0,
        concat_axis=0,
        tiled=True,
    )
    total_mean = jnp.sum(received, axis=0) / groups
    piece_momentum, new_group_server_error = compress(total_mean + group_server_error)
    shard_momentum = lax.all_gather(piece_momentum, "group", axis=0, tiled=True)
    new_momentum = lax.all_gather(shard_momentum, "node", axis=0, tiled=True)
    new_params = params - 0.05 * new_momentum / (jnp.sqrt(variance) + 1e-08)
    return (
        new_params,
        new_momentum,
        new_worker_error[None, None],
        new_server_error[None],
        new_group_worker_error[None],
        new_group_server_error,
    )


def solution(mesh):
    in_specs = (
        P("node", "group", None, None),
        P(),
        P(),
        P(),
        P("node", "group", None, None),
        P("group", "node", None),
        P("group", "node", None),
        P(("node", "group"), None),
    )
    out_specs = (
        P(),
        P(),
        P("node", "group", None, None),
        P("group", "node", None),
        P("group", "node", None),
        P(("node", "group"), None),
    )
    return jax.shard_map(body, mesh=mesh, in_specs=in_specs, out_specs=out_specs, check_vma=False)
```

profile of v0, /device:TPU:0, one launch (start us, length us, event | category | flops | bytes accessed | tf_op | source)
XLA Modules:
  0.0 60.1 jit_solution(13826548811941531077)
XLA Ops:
  0.6 1.5 %abs_reduce_fusion = (f32[128]{0:T(128)S(1)}, f32[128,1024]{1,0:T(8,128)S(1)}) fusion(f32[1,1,128,1024]{3,2,1,0:T(8,128)} %param.12, bf16[1,1,128,1024]{3,2,1,0:T(8,128)(2,1)} %param.8, f32[128,1024]{1,0:T(8,128)} %param.9), kind=kLoop, calls=%fused_computation.5 | loop fusion | flops 917376 | bytes 1835520 | tf_op jit(solution)/shard_map/reduce_sum | solution.py:8
  2.1 1.1 %subtract_bitcast_fusion = (f32[1,1,128,1024]{3,2,1,0:T(8,128)}, f32[128,1024]{1,0:T(8,128)}) fusion(f32[128,1024]{1,0:T(8,128)S(1)} %get-tuple-element.7, f32[128]{0:T(128)S(1)} %broadcast_multiply_fusion.4), kind=kLoop, calls=%fused_computation.2 | loop fusion | flops 393216 | bytes 1573376 | tf_op jit(solution)/shard_map/broadcast_in_dim | solution.py:51
  3.3 0.0 copy-start.1
  3.3 6.5 %all-to-all-start = ((f32[8,16,1024]{2,1,0:T(8,128)}), f32[8,16,1024]{2,1,0:T(8,128)S(1)}, u32[]{:S(2)}, u32[]{:S(2)}) async-start(f32[8,16,1024]{2,1,0:T(8,128)} %bitcast.2), calls=%async_computation | async-start | bytes 1048576 | tf_op jit(solution)/shard_map/all_to_all | solution.py:30
  9.7 0.0 copy-done.1
  9.8 0.0 copy-start
  9.8 0.8 %copy-done = f32[1,16,1024]{2,1,0:T(8,128)S(1)} copy-done((f32[1,16,1024]{2,1,0:T(8,128)S(1)}, f32[1,16,1024]{2,1,0:T(8,128)}, u32[]{:S(2)}) %copy-start) | copy-done | bytes 65560
  10.6 14.5 %all-to-all-done = f32[8,16,1024]{2,1,0:T(8,128)S(1)} async-done(((f32[8,16,1024]{2,1,0:T(8,128)}), f32[8,16,1024]{2,1,0:T(8,128)S(1)}, u32[]{:S(2)}, u32[]{:S(2)}) %all-to-all-start) | async-done | bytes 524320 | tf_op jit(solution)/shard_map/all_to_all | solution.py:30
  25.1 0.1 abs_reduce_fusion.1
  25.2 0.1 div.45
  25.3 0.2 fusion.1
  25.5 0.1 div.44
  25.6 0.7 %sign_multiply_fusion.2 = f32[4,4,1024]{2,1,0:T(4,128)} fusion(f32[4,4,1024]{2,1,0:T(4,128)S(1)} %squeeze.18, f32[4,4,1024]{2,1,0:T(4,128)S(1)} %div.46, f32[4,4,1024]{2,1,0:T(4,128)S(1)} %squeeze.17, f32[4,4]{1,0:T(4,128)S(1)} %div.45, f32[4,4]{1,0:T(4,128)S(1)} %div.44), kind=kLoop, calls=%fused_computation.14 | loop fusion | flops 98304 | bytes 262272 | tf_op jit(solution)/shard_map/mul | solution.py:9
  26.4 0.0 copy-start.4
  26.4 3.8 %all-to-all-start.1 = ((f32[4,4,1024]{2,1,0:T(4,128)}), f32[4,4,1024]{2,1,0:T(4,128)S(1)}, u32[]{:S(2)}, u32[]{:S(2)}) async-start(f32[4,4,1024]{2,1,0:T(4,128)} %sign_multiply_fusion.2), calls=%async_computation.1 | async-start | bytes 131072 | tf_op jit(solution)/shard_map/all_to_all | solution.py:36
  30.2 0.0 copy-start.3
  30.2 0.7 %multiply_subtract_fusion = (f32[1,16,1024]{2,1,0:T(8,128)}, f32[1,16,1024]{2,1,0:T(8,128)}) fusion(f32[1,16,1024]{2,1,0:T(8,128)S(1)} %copy-done.1, f32[16]{0:T(128)S(1)} %broadcast_multiply_fusion.2, f32[16]{0:T(128)S(1)} %broadcast_multiply_fusion.3, f32[1,16,1024]{2,1,0:T(8,128)S(1)} %copy-done, f32[16,1024]{1,0:T(8,128)S(1)} %reduce_sum.55), kind=kLoop, calls=%fused_computation.11 | loop fusion | flops 147456 | bytes 327808 | tf_op jit(solution)/shard_map/sub | solution.py:10
  31.0 0.0 copy-start.2
  31.0 4.1 %all-to-all-done.1 = f32[4,4,1024]{2,1,0:T(4,128)S(1)} async-done(((f32[4,4,1024]{2,1,0:T(4,128)}), f32[4,4,1024]{2,1,0:T(4,128)S(1)}, u32[]{:S(2)}, u32[]{:S(2)}) %all-to-all-start.1) | async-done | bytes 65568 | tf_op jit(solution)/shard_map/all_to_all | solution.py:36
  35.1 0.0 copy-done.4
  35.1 0.1 abs_reduce_fusion.2
  35.2 0.7 %fusion.3 = (f32[4,1024]{1,0:T(4,128)}, f32[1,4,1024]{2,1,0:T(4,128)S(1)}) fusion(f32[4]{0:T(128)S(1)} %broadcast_multiply_fusion.1, f32[4,1024]{1,0:T(4,128)S(1)} %copy-done.4, f32[4,1024]{1,0:T(4,128)S(1)} %reduce_sum.58), kind=kLoop, calls=%fused_computation.18 | loop fusion | flops 20480 | bytes 65552 | tf_op jit(solution)/shard_map/sub | solution.py:10
  35.9 7.5 %all-gather = f32[4,4,1024]{2,1,0:T(4,128)S(1)} all-gather(f32[1,4,1024]{2,1,0:T(4,128)S(1)} %get-tuple-element.15), channel_id=1, replica_groups=mesh['node'=8,'group'=4] {'group'}, dimensions={0}, use_global_device_ids=true | all-gather | bytes 81920 | tf_op jit(solution)/shard_map/all_gather | solution.py:45
  43.4 14.8 %all_gather.7 = f32[128,1024]{1,0:T(8,128)S(1)} all-gather(f32[16,1024]{1,0:T(8,128)S(1)} %reshape.89), channel_id=1, replica_groups=mesh['node'=8,'group'=4] {'node'}, dimensions={0}, use_global_device_ids=true | all-gather | bytes 589824 | tf_op jit(solution)/shard_map/all_gather | solution.py:46
  58.3 0.0 copy-done.3
  58.3 0.0 copy-done.2
  58.3 1.0 %divide_subtract_fusion = f32[128,1024]{1,0:T(8,128)} fusion(f32[128,1024]{1,0:T(8,128)S(1)} %copy-done.2, f32[128,1024]{1,0:T(8,128)S(1)} %copy-done.3, f32[128,1024]{1,0:T(8,128)S(1)} %all_gather.7), kind=kLoop, calls=%fused_computation.3 | loop fusion | flops 524288 | bytes 2097152 | tf_op jit(solution)/shard_map/sub | solution.py:47
  59.3 0.8 %copy.15 = f32[128,1024]{1,0:T(8,128)} copy(f32[128,1024]{1,0:T(8,128)S(1)} %all_gather.7) | data formatting | bytes 1048576
  (10 shorter events, 0.2 us)
Async XLA Ops:
  3.3 6.5 %copy-start.1 = (f32[1,16,1024]{2,1,0:T(8,128)S(1)}, f32[1,16,1024]{2,1,0:T(8,128)}, u32[]{:S(2)}) copy-start(f32[1,16,1024]{2,1,0:T(8,128)} %param.14) | copy-start | bytes 196612
  3.3 21.8 %all-to-all-start = ((f32[8,16,1024]{2,1,0:T(8,128)}), f32[8,16,1024]{2,1,0:T(8,128)S(1)}, u32[]{:S(2)}, u32[]{:S(2)}) async-start(f32[8,16,1024]{2,1,0:T(8,128)} %bitcast.2), calls=%async_computation | async-start | bytes 1048576 | tf_op jit(solution)/shard_map/all_to_all | solution.py:30
  9.8 0.8 %copy-start = (f32[1,16,1024]{2,1,0:T(8,128)S(1)}, f32[1,16,1024]{2,1,0:T(8,128)}, u32[]{:S(2)}) copy-start(f32[1,16,1024]{2,1,0:T(8,128)} %param.13) | copy-start | bytes 196612
  26.4 8.7 %copy-start.4 = (f32[4,1024]{1,0:T(4,128)S(1)}, f32[4,1024]{1,0:T(4,128)}, u32[]{:S(2)}) copy-start(f32[4,1024]{1,0:T(4,128)} %param.15) | copy-start | bytes 49156
  26.4 8.7 %all-to-all-start.1 = ((f32[4,4,1024]{2,1,0:T(4,128)}), f32[4,4,1024]{2,1,0:T(4,128)S(1)}, u32[]{:S(2)}, u32[]{:S(2)}) async-start(f32[4,4,1024]{2,1,0:T(4,128)} %sign_multiply_fusion.2), calls=%async_computation.1 | async-start | bytes 131072 | tf_op jit(solution)/shard_map/all_to_all | solution.py:36
  30.2 28.0 %copy-start.3 = (f32[128,1024]{1,0:T(8,128)S(1)}, f32[128,1024]{1,0:T(8,128)}, u32[]{:S(2)}) copy-start(f32[128,1024]{1,0:T(8,128)} %param.10) | copy-start | bytes 1572868
  31.0 27.3 %copy-start.2 = (f32[128,1024]{1,0:T(8,128)S(1)}, f32[128,1024]{1,0:T(8,128)}, u32[]{:S(2)}) copy-start(f32[128,1024]{1,0:T(8,128)} %param.11) | copy-start | bytes 1572868
where the time goes:
time: 60.5 us; the launch traced here: 60.1 us
  blocking collectives  22.3 us (37%)
  waiting for transfers between devices  18.6 us (31%)
  starting transfers between devices  10.3 us (17%)
  other arithmetic  6.3 us (10%)
  local copies, waits for them, and re-layouts  1.88 us (3%)
  between operations  0.69 us (1%)
    all_gather x1, blocking collectives, body(): new_momentum = lax.all_gather(shard_momentum, 'node', axis=0, tiled=True)  14.8 us
    all_to_all x1, waiting for transfers between devices, body(): lax.all_to_all(first.reshape(nodes, shard_rows, width), 'node', split_axi...  14.5 us
    all_gather x1, blocking collectives, body(): shard_momentum = lax.all_gather(piece_momentum, 'group', axis=0, tiled=True)  7.45 us
    all_to_all x1, starting transfers between devices, body(): lax.all_to_all(first.reshape(nodes, shard_rows, width), 'node', split_axi...  6.49 us
    all_to_all x1, waiting for transfers between devices, body(): lax.all_to_all(second.reshape(groups, shard_rows // groups, width), 'grou...  4.11 us
    all_to_all x1, starting transfers between devices, body(): lax.all_to_all(second.reshape(groups, shard_rows // groups, width), 'grou...  3.85 us
    reduce_sum x4, other arithmetic, compress(): scale = jnp.mean(jnp.abs(values), axis=-1, keepdims=True)  1.92 us
    unnamed x12, local copies, waits for them, and re-layouts  1.64 us
  transfers between devices with their start and end apart: 2, of which 2 were waited for; matrix products, arithmetic and copies ran while one was open for 1% of the time, Pallas kernels for 0%

commit v1 on v0

v1 whole, which is shorter than its diff:
```python
import functools

import jax
import jax.numpy as jnp
from jax import lax
from jax.experimental import pallas as pl
from jax.experimental.pallas import tpu as pltpu
from jax.sharding import PartitionSpec as P

CORES = 2
VMEM = pl.BlockSpec(memory_space=pltpu.VMEM)
HBM = pl.BlockSpec(memory_space=pltpu.HBM)


def paired(size):
    return size & (size - 1) == 0


def target(index, step, size):
    if paired(size):
        return index ^ step
    return lax.rem(index + step, size) if not isinstance(index, int) else (index + step) % size


def source(index, step, size):
    return index ^ step if paired(size) else lax.rem(index + (size - step), size)


def steps_of(size):
    if not paired(size):
        return list(range(1, size))
    steps, half = [], size // 2
    while half:
        steps += range(half, 2 * half)
        half //= 2
    return steps


def packed_of(values, width):
    scale = jnp.sum(jnp.abs(values), axis=-1, keepdims=True) / width
    return jnp.where(values > 0, scale, jnp.where(values < 0, -scale, jnp.zeros_like(values)))


def swap_cores(values, nodes):
    return lax.ppermute(values, "node", [(i, i ^ 1) for i in range(nodes)])


def send_chip(values, step, nodes):
    chips = nodes // CORES
    pairs = [
        (CORES * i + core, CORES * target(i, step, chips) + 1 - core) for i in range(chips) for core in range(CORES)
    ]
    return lax.ppermute(values, "node", pairs)


def send_group(values, step, groups):
    return lax.ppermute(values, "group", [(i, target(i, step, groups)) for i in range(groups)])


def vmem(*shape):
    return pltpu.VMEM(shape, jnp.float32)


def near(*values):
    return [pltpu.with_memory_space_constraint(value, pltpu.VMEM) for value in values]


def far(*values):
    return [pltpu.with_memory_space_constraint(value, pltpu.HBM) for value in values]


def room(*scratch):
    return pltpu.CompilerParams(vmem_limit_bytes=sum(scratch) + (4 << 20))


def place_of():
    node = lax.axis_index("node")
    return node // CORES, lax.rem(node, CORES)


def head_kernel(order, gradient, momentum, worker_error, *rest):
    chips = len(order)
    small, rest = rest[:3], rest[3:]
    kept, (sooner, later, error, *near_small, g_buf, m_buf, w_buf, sems, small_sems) = rest[:chips], rest[chips:]
    rows, width = momentum.shape
    chip_rows = rows // chips
    shard_rows = chip_rows // CORES
    chip, core = place_of()
    copies = []
    for at, step in enumerate(order):
        where = target(chip, step, chips)
        part = pl.ds(pl.multiple_of(where * chip_rows, chip_rows), chip_rows)
        pairs = ((gradient.at[0, 0], g_buf), (momentum, m_buf), (worker_error.at[0, 0], w_buf))
        three = [
            pltpu.make_async_copy(src.at[part], dst.at[at], sems.at[at, kind]) for kind, (src, dst) in enumerate(pairs)
        ]
        for copy in three:
            copy.start()
        copies.append((where, three))
    brought = [pltpu.make_async_copy(src, dst, small_sems.at[i]) for i, (src, dst) in enumerate(zip(small, near_small))]
    for copy in brought:
        copy.start()
    for at, (where, three) in enumerate(copies):
        for copy in three:
            copy.wait()
        mine = core if order[at] == 0 else 1 - core
        for side, half in enumerate((mine, 1 - mine)):
            some = pl.ds(pl.multiple_of(half * shard_rows, shard_rows), shard_rows)
            local = 0.9 * m_buf[at, some] + 0.1 * g_buf[at, some].astype(jnp.float32) + w_buf[at, some]
            first = packed_of(local, width)
            if side == 0:
                kept[at][...] = first
            elif at == 0:
                sooner[...] = first
            else:
                later[at - 1] = first
            start = pl.multiple_of(where * chip_rows + half * shard_rows, shard_rows)
            error[pl.ds(start, shard_rows), :] = local - first
    for copy in brought:
        copy.wait()


def head(gradient, momentum, worker_error, small, order):
    rows, width = momentum.shape
    chips = len(order)
    chip_rows = rows // chips
    shard = (chip_rows // CORES, width)
    return pl.pallas_call(
        functools.partial(head_kernel, order),
        out_shape=[vmem(*shard)] * (chips + 1) + [vmem(chips - 1, *shard), vmem(rows, width)] + [vmem(*x.shape) for x in small],
        in_specs=[HBM] * 6,
        out_specs=[VMEM] * (chips + 6),
        scratch_shapes=[
            pltpu.VMEM((chips, chip_rows, width), gradient.dtype),
            pltpu.VMEM((chips, chip_rows, width), jnp.float32),
            pltpu.VMEM((chips, chip_rows, width), jnp.float32),
            pltpu.SemaphoreType.DMA((chips, 3)),
            pltpu.SemaphoreType.DMA((3,)),
        ],
        compiler_params=room(gradient.nbytes, momentum.nbytes, worker_error.nbytes),
    )(*far(gradient, momentum, worker_error, *small))


def server_kernel(nodes, count, *refs):
    parts, (server, worker, second, error_0, error_1) = refs[:count], refs[count:]
    width = server.shape[-1]
    total = parts[0][...]
    for other in parts[1:]:
        total = total + other[...]
    values = total / nodes + server[...]
    group_q = packed_of(values, width)
    error_0[...] = values - group_q
    values = group_q + worker[...]
    result = packed_of(values, width)
    second[...] = result
    error_1[...] = values - result


def serve(parts, server, worker, nodes):
    return pl.pallas_call(
        functools.partial(server_kernel, nodes, len(parts)),
        out_shape=[vmem(*server.shape)] * 3,
        in_specs=[VMEM] * (len(parts) + 2),
        out_specs=[VMEM] * 3,
        compiler_params=room(),
    )(*near(*parts, server, worker))


def store_kernel(count, *refs):
    sems = refs[-1]
    copies = [pltpu.make_async_copy(refs[i], refs[count + i], sems.at[i]) for i in range(count)]
    for copy in copies:
        copy.start()
    for copy in copies:
        copy.wait()


def store(*values):
    count = len(values)
    return pl.pallas_call(
        functools.partial(store_kernel, count),
        out_shape=[pltpu.HBM(value.shape, jnp.float32) for value in values],
        in_specs=[VMEM] * count,
        out_specs=[HBM] * count,
        scratch_shapes=[pltpu.SemaphoreType.DMA((count,))],
        compiler_params=room(),
    )(*near(*values))


def average_kernel(groups, *refs):
    parts, (server, result, error) = refs[:groups], refs[groups:]
    width = server.shape[-1]
    total = parts[0][...]
    for other in parts[1:]:
        total = total + other[...]
    values = total / groups + server[...]
    packed = packed_of(values, width)
    result[...] = packed
    error[...] = values - packed


def average(parts, server):
    return pl.pallas_call(
        functools.partial(average_kernel, len(parts)),
        out_shape=[vmem(*server.shape)] * 2,
        in_specs=[VMEM] * (len(parts) + 1),
        out_specs=[VMEM] * 2,
        compiler_params=room(),
    )(*near(*parts, server))


def update_kernel(steps, chips, *refs):
    count = len(steps)
    mine, given, (variance, params) = refs[:count], refs[count : 2 * count], refs[2 * count : 2 * count + 2]
    new_params, new_momentum, p_buf, m_buf, sems = refs[-5:]
    shard_rows = mine[0].shape[0]
    chip_rows = CORES * shard_rows
    chip, core = place_of()
    copies = []
    for at, step in enumerate(steps):
        part = pl.ds(pl.multiple_of(source(chip, step, chips) * chip_rows, chip_rows), chip_rows)
        half = core if step == 0 else 1 - core
        for values, side in ((mine[at], half), (given[at], 1 - half)):
            m_buf[at, pl.ds(pl.multiple_of(side * shard_rows, shard_rows), shard_rows), :] = values[...]
        copies.append(pltpu.make_async_copy(m_buf.at[at], new_momentum.at[part], sems.at[at, 0]))
        copies[-1].start()
        p_buf[at] = params[part, :] - 0.05 * m_buf[at] / (jnp.sqrt(variance[part, :]) + 1e-08)
        copies.append(pltpu.make_async_copy(p_buf.at[at], new_params.at[part], sems.at[at, 1]))
        copies[-1].start()
    for copy in copies:
        copy.wait()


def update(mine, given, variance, params, so_far, steps, chips):
    shard_rows, width = mine[0].shape
    count = len(steps)
    buffer = (count, CORES * shard_rows, width)
    return pl.pallas_call(
        functools.partial(update_kernel, steps, chips),
        out_shape=[pltpu.HBM(params.shape, jnp.float32)] * 2,
        in_specs=[VMEM] * (2 * count + 2) + [HBM] * len(so_far),
        out_specs=[HBM] * 2,
        scratch_shapes=[
            pltpu.VMEM(buffer, jnp.float32),
            pltpu.VMEM(buffer, jnp.float32),
            pltpu.SemaphoreType.DMA((count, 2)),
        ],
        input_output_aliases={2 * count + 2 + i: i for i in range(len(so_far))},
        compiler_params=room(2 * count * CORES * mine[0].nbytes),
    )(*near(*mine, *given, variance, params), *so_far)


def body(
    gradient,
    momentum,
    variance,
    params,
    worker_error,
    server_error,
    group_worker_error,
    group_server_error,
):
    nodes = lax.axis_size("node")
    groups = lax.axis_size("group")
    chips = nodes // CORES
    rows, width = momentum.shape
    shard_rows = rows // nodes
    piece_rows = group_server_error.shape[0]
    group = lax.axis_index("group")
    along = steps_of(chips)
    across = steps_of(groups)

    small = (server_error[0], group_worker_error[0], group_server_error)
    *kept, sooner, later, error, server, worker, own_piece = head(gradient, momentum, worker_error, small, along + [0])
    got = [swap_cores(sooner, nodes)]
    got += list(swap_cores(later, nodes))
    parts = [kept[-1], got[-1]]
    for at, step in enumerate(along):
        parts.append(send_chip(kept[at] + got[at], step, nodes))

    got_pieces = []
    for step in across:
        got_pieces.append(send_group(own_piece, step, groups))

    second, error_0, error_1 = serve(parts, server, worker, nodes)
    error_0, got_pieces = lax.optimization_barrier((error_0, got_pieces))
    pieces = jnp.zeros((groups, piece_rows, width), jnp.float32)
    for step, piece in zip([0] + across, [own_piece] + got_pieces):
        pieces = lax.dynamic_update_slice_in_dim(pieces, piece[None], source(group, step, groups), 0)
    seconds = [second]
    for step in across:
        seconds.append(send_group(second, step, groups))
    new_worker_error, new_server_error, new_group_worker_error = store(error[None, None], error_0[None], error_1[None])

    mine, shard_error = average(seconds, pieces.reshape(shard_rows, width))
    new_group_server_error = lax.dynamic_slice_in_dim(shard_error, group * piece_rows, piece_rows, 0)

    arrived = [mine]
    for step in along:
        arrived.append(send_chip(mine, step, nodes))
    given = []
    for step, values in zip([0] + along, arrived):
        given.append(swap_cores(values, nodes))
    outs = ()
    for some in (slice(0, 1), slice(1, chips - 1), slice(chips - 1, chips)):
        outs = update(arrived[some], given[some], variance, params, outs, ([0] + along)[some], chips)
    new_params, new_momentum = outs
    return (
        new_params,
        new_momentum,
        new_worker_error,
        new_server_error,
        new_group_worker_error,
        new_group_server_error,
    )


def solution(mesh):
    in_specs = (
        P("node", "group", None, None),
        P(),
        P(),
        P(),
        P("node", "group", None, None),
        P("group", "node", None),
        P("group", "node", None),
        P(("node", "group"), None),
    )
    out_specs = (
        P(),
        P(),
        P("node", "group", None, None),
        P("group", "node", None),
        P("group", "node", None),
        P(("node", "group"), None),
    )
    return jax.shard_map(body, mesh=mesh, in_specs=in_specs, out_specs=out_specs, check_vma=False)
```

time: 60.5 us -> 40.5 us (0.67)
  blocking collectives: 22.3 us -> 0 us
  starting transfers between devices: 10.3 us -> 23.7 us
  waiting for transfers between devices: 18.6 us -> 9.86 us
  other arithmetic: 6.3 us -> 0.02 us
  Pallas kernels: 0 us -> 5.24 us
  local copies, waits for them, and re-layouts: 1.88 us -> 0.71 us
    ppermute x0 -> x18, starting transfers between devices: none -> 23.7 us  [the longest x6 13.4 us: send_chip(): return lax.ppermute(values, 'node', pairs)]
    all_gather x2 -> x0, blocking collectives: 22.3 us -> none  [the longest x1 14.8 us: body(): new_momentum = lax.all_gather(shard_momentum, 'node', axis=0, tiled=True)]
    all_to_all x2 -> x0, waiting for transfers between devices: 18.6 us -> none  [the longest x1 14.5 us: body(): lax.all_to_all(first.reshape(nodes, shard_rows, width), 'node', split_axi...]
    all_to_all x2 -> x0, starting transfers between devices: 10.3 us -> none  [the longest x1 6.49 us: body(): lax.all_to_all(first.reshape(nodes, shard_rows, width), 'node', split_axi...]
    ppermute x0 -> x18, waiting for transfers between devices: none -> 9.86 us  [the longest x6 5.24 us: send_chip(): return lax.ppermute(values, 'node', pairs)]
    pallas_call x0 -> x7, Pallas kernels: none -> 5.24 us  [the longest x3 2.38 us: update(): pl.pallas_call(functools.partial(update_kernel, steps, chips), out_shape=...]
    sub x3 -> x0, other arithmetic: 2.42 us -> none  [the longest x2 1.41 us: compress(): return (packed, values - packed)]
    reduce_sum x6 -> x0, other arithmetic: 1.97 us -> none  [the longest x4 1.92 us: compress(): scale = jnp.mean(jnp.abs(values), axis=-1, keepdims=True)]
  transfers between devices with their start and end apart: 2 -> 18, of which waited for: 2 -> 7; matrix products, arithmetic and copies ran while one was open for 1% -> 2% of each run, Pallas kernels for 0% -> 7%
where the time goes in v1:
time: 40.5 us; the launch traced here: 40.3 us
  starting transfers between devices  23.7 us (59%)
  waiting for transfers between devices  9.86 us (24%)
  Pallas kernels  5.24 us (13%)
  between operations  0.8 us (2%)
  local copies, waits for them, and re-layouts  0.71 us (2%)
    ppermute x6, starting transfers between devices, send_chip(): return lax.ppermute(values, 'node', pairs)  13.4 us
    ppermute x6, starting transfers between devices, send_group(): lax.ppermute(values, 'group', [(i, target(i, step, groups)) for i in rang...  8.13 us
    ppermute x6, waiting for transfers between devices, send_chip(): return lax.ppermute(values, 'node', pairs)  5.24 us
    ppermute x6, waiting for transfers between devices, send_group(): lax.ppermute(values, 'group', [(i, target(i, step, groups)) for i in rang...  3.63 us
    pallas_call x3, Pallas kernels, update(): pl.pallas_call(functools.partial(update_kernel, steps, chips), out_shape=...  2.38 us
    ppermute x6, starting transfers between devices, swap_cores(): return lax.ppermute(values, 'node', [(i, i ^ 1) for i in range(nodes)])  2.11 us
    pallas_call x1, Pallas kernels, head(): pl.pallas_call(functools.partial(head_kernel, order), out_shape=[vmem(*sh...  1.71 us
    ppermute x6, waiting for transfers between devices, swap_cores(): return lax.ppermute(values, 'node', [(i, i ^ 1) for i in range(nodes)])  0.99 us
  transfers between devices with their start and end apart: 18, of which 7 were waited for; matrix products, arithmetic and copies ran while one was open for 2% of the time, Pallas kernels for 7%

profile of v1, /device:TPU:0, one launch (start us, length us, event | category | flops | bytes accessed | tf_op | source)
XLA Modules:
  0.0 40.3 jit_solution(11244436941792433166)
XLA Ops:
  0.6 1.7 %shard_map.127 = (f32[16,1024]{1,0:T(8,128)S(1)}, f32[16,1024]{1,0:T(8,128)S(1)}, f32[16,1024]{1,0:T(8,128)S(1)}, f32[16,1024]{1,0:T(8,128)S(1)}, f32[16,1024]{1...) custom-call(bf16[1,1,128,1024]{3,2,1,0:T(8,128)(2,1)} %gradient.1, ...), custom_call_target="tpu_custom_call" | custom-call | tf_op jit(solution)/shard_map/pallas_call | solution.py:128
  2.3 3.0 %collective-permute-start.10 = (f32[4,1024]{1,0:T(4,128)S(1)}, f32[4,1024]{1,0:T(4,128)S(1)}, u32[]{:S(2)}, u32[]{:S(2)}) collective-permute-start(f32[4,1024]{1,0:T(4,128)S(1)} %get-tuple-element.43), channel_id=1, source_target_pairs={{0,1},{1,0},{2,3},{3,2},{4,5},{5,4},{6,7},{7,6},{8,9},{9,8},{10,11... | collective-permute-start | bytes 49160 | tf_op jit(solution)/shard_map/ppermute | solution.py:57
  5.4 1.5 %collective-permute-start.8 = (f32[4,1024]{1,0:T(4,128)S(1)}, f32[4,1024]{1,0:T(4,128)S(1)}, u32[]{:S(2)}, u32[]{:S(2)}) collective-permute-start(f32[4,1024]{1,0:T(4,128)S(1)} %get-tuple-element.43), channel_id=1, source_target_pairs={{0,2},{1,3},{2,0},{3,1},{4,6},{5,7},{6,4},{7,5},{8,10},{9,11},{10,... | collective-permute-start | bytes 49160 | tf_op jit(solution)/shard_map/ppermute | solution.py:57
  6.9 0.0 collective-permute-start.9
  6.9 0.0 collective-permute-start
  6.9 0.5 %collective-permute-start.1 = (f32[16,1024]{1,0:T(8,128)S(1)}, f32[16,1024]{1,0:T(8,128)S(1)}, u32[]{:S(2)}, u32[]{:S(2)}) collective-permute-start(f32[16,1024]{1,0:T(8,128)S(1)} %get-tuple-element.37), channel_id=1, source_target_pairs={{0,4},{4,0},{8,12},{12,8},{16,20},{20,16},{24,28},{28,24},{1,5},{5... | collective-permute-start | bytes 196616 | tf_op jit(solution)/shard_map/ppermute | solution.py:45
  7.5 1.0 %collective-permute-done.1 = f32[16,1024]{1,0:T(8,128)S(1)} collective-permute-done((f32[16,1024]{1,0:T(8,128)S(1)}, f32[16,1024]{1,0:T(8,128)S(1)}, u32[]{:S(2)}, u32[]{:S(2)}) %collective-permute-start.1) | collective-permute-done | bytes 65568 | tf_op jit(solution)/shard_map/ppermute | solution.py:45
  8.5 2.9 %collective-permute-start.2 = (f32[16,1024]{1,0:T(8,128)S(1)}, f32[16,1024]{1,0:T(8,128)S(1)}, u32[]{:S(2)}, u32[]{:S(2)}) collective-permute-start(f32[16,1024]{1,0:T(8,128)S(1)} %add.24), channel_id=1, source_target_pairs={{0,20},{4,16},{8,28},{12,24},{16,4},{20,0},{24,12},{28,8},{1,21},{... | collective-permute-start | bytes 196616 | tf_op jit(solution)/shard_map/ppermute | solution.py:53
  11.4 0.0 collective-permute-done
  11.4 1.3 %collective-permute-start.3 = (f32[16,1024]{1,0:T(8,128)S(1)}, f32[16,1024]{1,0:T(8,128)S(1)}, u32[]{:S(2)}, u32[]{:S(2)}) collective-permute-start(f32[16,1024]{1,0:T(8,128)S(1)} %get-tuple-element.63), channel_id=1, source_target_pairs={{0,28},{4,24},{8,20},{12,16},{16,12},{20,8},{24,4},{28,0},{1,29},{... | collective-permute-start | bytes 196616 | tf_op jit(solution)/shard_map/ppermute | solution.py:53
  12.7 0.9 %collective-permute-done.2.refs_2_ = f32[16,1024]{1,0:T(8,128)S(1)} collective-permute-done((f32[16,1024]{1,0:T(8,128)S(1)}, f32[16,1024]{1,0:T(8,128)S(1)}, u32[]{:S(2)}, u32[]{:S(2)}) %collective-permute-start.2) | collective-permute-done | bytes 65568 | tf_op jit(solution)/shard_map/ppermute | solution.py:53
  13.6 3.8 %collective-permute-start.4 = (f32[16,1024]{1,0:T(8,128)S(1)}, f32[16,1024]{1,0:T(8,128)S(1)}, u32[]{:S(2)}, u32[]{:S(2)}) collective-permute-start(f32[16,1024]{1,0:T(8,128)S(1)} %get-tuple-element.62), channel_id=1, source_target_pairs={{0,12},{4,8},{8,4},{12,0},{16,28},{20,24},{24,20},{28,16},{1,13},{... | collective-permute-start | bytes 196616 | tf_op jit(solution)/shard_map/ppermute | solution.py:53
  17.5 0.0 collective-permute-done.3.refs_3_
  17.5 2.2 %collective-permute-done.4.refs_4_ = f32[16,1024]{1,0:T(8,128)S(1)} collective-permute-done((f32[16,1024]{1,0:T(8,128)S(1)}, f32[16,1024]{1,0:T(8,128)S(1)}, u32[]{:S(2)}, u32[]{:S(2)}) %collective-permute-start.4) | collective-permute-done | bytes 65568 | tf_op jit(solution)/shard_map/ppermute | solution.py:53
  19.7 0.2 shard_map.128
  19.9 1.6 %collective-permute-start.5 = (f32[16,1024]{1,0:T(8,128)S(1)}, f32[16,1024]{1,0:T(8,128)S(1)}, u32[]{:S(2)}, u32[]{:S(2)}) collective-permute-start(f32[16,1024]{1,0:T(8,128)S(1)} %get-tuple-element.42.refs_0_), channel_id=1, source_target_pairs={{0,2},{1,3},{2,0},{3,1},{4,6},{5,7},{6,4},{7,5},{8,10},{9,11},{10,... | collective-permute-start | bytes 196616 | tf_op jit(solution)/shard_map/ppermute | solution.py:57
  21.5 1.4 %collective-permute-start.6 = (f32[16,1024]{1,0:T(8,128)S(1)}, f32[16,1024]{1,0:T(8,128)S(1)}, u32[]{:S(2)}, u32[]{:S(2)}) collective-permute-start(f32[16,1024]{1,0:T(8,128)S(1)} %get-tuple-element.42.refs_0_), channel_id=1, source_target_pairs={{0,3},{1,2},{2,1},{3,0},{4,7},{5,6},{6,5},{7,4},{8,11},{9,10},{10,... | collective-permute-start | bytes 196616 | tf_op jit(solution)/shard_map/ppermute | solution.py:57
  22.9 0.0 collective-permute-done.10
  22.9 0.5 %collective-permute-start.7 = (f32[16,1024]{1,0:T(8,128)S(1)}, f32[16,1024]{1,0:T(8,128)S(1)}, u32[]{:S(2)}, u32[]{:S(2)}) collective-permute-start(f32[16,1024]{1,0:T(8,128)S(1)} %get-tuple-element.42.refs_0_), channel_id=1, source_target_pairs={{0,1},{1,0},{2,3},{3,2},{4,5},{5,4},{6,7},{7,6},{8,9},{9,8},{10,11... | collective-permute-start | bytes 196616 | tf_op jit(solution)/shard_map/ppermute | solution.py:57
  23.5 0.0 collective-permute-done.8
  23.5 0.0 collective-permute-done.9
  23.5 0.0 copy-start.1
  23.6 0.0 copy-start
  23.6 0.7 %collective-permute-done.5.refs_1_ = f32[16,1024]{1,0:T(8,128)S(1)} collective-permute-done((f32[16,1024]{1,0:T(8,128)S(1)}, f32[16,1024]{1,0:T(8,128)S(1)}, u32[]{:S(2)}, u32[]{:S(2)}) %collective-permute-start.5) | collective-permute-done | bytes 65568 | tf_op jit(solution)/shard_map/ppermute | solution.py:57
  24.2 2.9 %collective-permute-done.6.refs_2_ = f32[16,1024]{1,0:T(8,128)S(1)} collective-permute-done((f32[16,1024]{1,0:T(8,128)S(1)}, f32[16,1024]{1,0:T(8,128)S(1)}, u32[]{:S(2)}, u32[]{:S(2)}) %collective-permute-start.6) | collective-permute-done | bytes 65568 | tf_op jit(solution)/shard_map/ppermute | solution.py:57
  27.2 0.0 collective-permute-done.7.refs_3_
  27.2 0.1 shard_map.129
  27.3 2.3 %collective-permute-start.13 = (f32[16,1024]{1,0:T(8,128)S(1)}, f32[16,1024]{1,0:T(8,128)S(1)}, u32[]{:S(2)}, u32[]{:S(2)}) collective-permute-start(f32[16,1024]{1,0:T(8,128)S(1)} %get-tuple-element.48.refs_0_), channel_id=1, source_target_pairs={{0,20},{4,16},{8,28},{12,24},{16,4},{20,0},{24,12},{28,8},{1,21},{... | collective-permute-start | bytes 196616 | tf_op jit(solution)/shard_map/ppermute | solution.py:53
  29.6 2.2 %collective-permute-start.14 = (f32[16,1024]{1,0:T(8,128)S(1)}, f32[16,1024]{1,0:T(8,128)S(1)}, u32[]{:S(2)}, u32[]{:S(2)}) collective-permute-start(f32[16,1024]{1,0:T(8,128)S(1)} %get-tuple-element.48.refs_0_), channel_id=1, source_target_pairs={{0,28},{4,24},{8,20},{12,16},{16,12},{20,8},{24,4},{28,0},{1,29},{... | collective-permute-start | bytes 196616 | tf_op jit(solution)/shard_map/ppermute | solution.py:53
  31.8 0.9 %collective-permute-start.11 = (f32[16,1024]{1,0:T(8,128)S(1)}, f32[16,1024]{1,0:T(8,128)S(1)}, u32[]{:S(2)}, u32[]{:S(2)}) collective-permute-start(f32[16,1024]{1,0:T(8,128)S(1)} %get-tuple-element.48.refs_0_), channel_id=1, source_target_pairs={{0,12},{4,8},{8,4},{12,0},{16,28},{20,24},{24,20},{28,16},{1,13},{... | collective-permute-start | bytes 196616 | tf_op jit(solution)/shard_map/ppermute | solution.py:53
  32.7 0.8 %shard_map.133 = (f32[1,1,128,1024]{3,2,1,0:T(8,128)}, f32[1,16,1024]{2,1,0:T(8,128)}, f32[1,16,1024]{2,1,0:T(8,128)}) custom-call(f32[1,1,128,1024]{3,2,1,0:T(8,128)S(1)} %bitcast.23, f32[1,16,1024]{2,1,0:T(8,128)S(1)} %bitcast.24, f32[1,16,1024]{2,1,0:T(8,128)S(1)} %bitcast.25), custom_call_target="tpu_custom_call" | custom-call | tf_op jit(solution)/shard_map/pallas_call | solution.py:180
  33.5 0.1 collective-permute-start.17
  33.6 0.0 collective-permute-done.13.refs_0_
  33.6 0.5 %collective-permute-start.15 = (f32[16,1024]{1,0:T(8,128)S(1)}, f32[16,1024]{1,0:T(8,128)S(1)}, u32[]{:S(2)}, u32[]{:S(2)}) collective-permute-start(f32[16,1024]{1,0:T(8,128)S(1)} %collective-permute-done.13.refs_0_), channel_id=1, source_target_pairs={{0,4},{4,0},{8,12},{12,8},{16,20},{20,16},{24,28},{28,24},{1,5},{5... | collective-permute-start | bytes 196616 | tf_op jit(solution)/shard_map/ppermute | solution.py:45
  34.1 1.4 %collective-permute-done.14.refs_1_ = f32[16,1024]{1,0:T(8,128)S(1)} collective-permute-done((f32[16,1024]{1,0:T(8,128)S(1)}, f32[16,1024]{1,0:T(8,128)S(1)}, u32[]{:S(2)}, u32[]{:S(2)}) %collective-permute-start.14) | collective-permute-done | bytes 65568 | tf_op jit(solution)/shard_map/ppermute | solution.py:53
  35.5 0.8 %collective-permute-start.16 = (f32[16,1024]{1,0:T(8,128)S(1)}, f32[16,1024]{1,0:T(8,128)S(1)}, u32[]{:S(2)}, u32[]{:S(2)}) collective-permute-start(f32[16,1024]{1,0:T(8,128)S(1)} %collective-permute-done.14.refs_1_), channel_id=1, source_target_pairs={{0,4},{4,0},{8,12},{12,8},{16,20},{20,16},{24,28},{28,24},{1,5},{5... | collective-permute-start | bytes 196616 | tf_op jit(solution)/shard_map/ppermute | solution.py:45
  36.3 0.7 %collective-permute-done.11.refs_0_ = f32[16,1024]{1,0:T(8,128)S(1)} collective-permute-done((f32[16,1024]{1,0:T(8,128)S(1)}, f32[16,1024]{1,0:T(8,128)S(1)}, u32[]{:S(2)}, u32[]{:S(2)}) %collective-permute-start.11) | collective-permute-done | bytes 65568 | tf_op jit(solution)/shard_map/ppermute | solution.py:53
  37.0 0.3 collective-permute-start.12
  37.3 0.6 %constant_dynamic-slice_fusion = f32[4,1024]{1,0:T(4,128)} fusion(f32[16,1024]{1,0:T(8,128)S(1)} %get-tuple-element.61, s32[]{:T(128)S(6)} %select_n.19), kind=kLoop, calls=%fused_computation.9 | loop fusion | bytes 32772 | tf_op jit(solution)/shard_map/dynamic_slice | solution.py:296
  37.9 0.0 collective-permute-done.17.refs_1_
  37.9 0.0 copy-done.1
  37.9 0.0 copy-done
  37.9 0.8 %shard_map.130 = (f32[128,1024]{1,0:T(8,128)}, f32[128,1024]{1,0:T(8,128)}) custom-call(f32[16,1024]{1,0:T(8,128)S(1)} %get-tuple-element.48.refs_0_, f32[16,1024]{1,0:T(8,128)S(1)} %collective-permute-done.17.refs_1_, f32[128,1024]{1,0:T(8,128)S(1)} %copy-done, f32[128,1024]{1,0:T(8,128)S(1)} %copy-done.1), custom_call_target="tpu_custom_call" | custom-call | tf_op jit(solution)/shard_map/pallas_call | solution.py:238
  38.6 0.0 collective-permute-done.15.refs_2_
  38.6 0.0 collective-permute-done.16.refs_3_
  38.7 0.9 %shard_map.131 = (f32[128,1024]{1,0:T(8,128)}, f32[128,1024]{1,0:T(8,128)}) custom-call(f32[16,1024]{1,0:T(8,128)S(1)} %collective-permute-done.13.refs_0_, f32[16,1024]{1,0:T(8,128)S(1)} %collective-permute-done.14.refs_1_, f32[16,1024]{1,0:T(8,128)S(1)} %collective-permute-done.15.refs_2_, ...), custom_call_target="tpu_custom_call", output_to_operand_aliasing={{0}: (6, {}), {1}: (7, {})} | custom-call | tf_op jit(solution)/shard_map/pallas_call | solution.py:238
  39.5 0.0 collective-permute-done.12.refs_1_
  39.5 0.8 %shard_map.132 = (f32[128,1024]{1,0:T(8,128)}, f32[128,1024]{1,0:T(8,128)}) custom-call(f32[16,1024]{1,0:T(8,128)S(1)} %collective-permute-done.11.refs_0_, f32[16,1024]{1,0:T(8,128)S(1)} %collective-permute-done.12.refs_1_, f32[128,1024]{1,0:T(8,128)S(1)} %copy-done, f32[128,1024]{1,0:T(8,128)S(1)} %copy-done.1, ...), custom_call_target="tpu_custom_call", output_to_operand_aliasing={{0}: (4, {}), {1}: (5, {})} | custom-call | tf_op jit(solution)/shard_map/pallas_call | solution.py:238
  (9 shorter events, 0.1 us)
Async XLA Ops:
  2.3 20.6 %collective-permute-start.10 = (f32[4,1024]{1,0:T(4,128)S(1)}, f32[4,1024]{1,0:T(4,128)S(1)}, u32[]{:S(2)}, u32[]{:S(2)}) collective-permute-start(f32[4,1024]{1,0:T(4,128)S(1)} %get-tuple-element.43), channel_id=1, source_target_pairs={{0,1},{1,0},{2,3},{3,2},{4,5},{5,4},{6,7},{7,6},{8,9},{9,8},{10,11... | collective-permute-start | bytes 49160 | tf_op jit(solution)/shard_map/ppermute | solution.py:57
  5.4 18.1 %collective-permute-start.8 = (f32[4,1024]{1,0:T(4,128)S(1)}, f32[4,1024]{1,0:T(4,128)S(1)}, u32[]{:S(2)}, u32[]{:S(2)}) collective-permute-start(f32[4,1024]{1,0:T(4,128)S(1)} %get-tuple-element.43), channel_id=1, source_target_pairs={{0,2},{1,3},{2,0},{3,1},{4,6},{5,7},{6,4},{7,5},{8,10},{9,11},{10,... | collective-permute-start | bytes 49160 | tf_op jit(solution)/shard_map/ppermute | solution.py:57
  6.9 16.6 %collective-permute-start.9 = (f32[4,1024]{1,0:T(4,128)S(1)}, f32[4,1024]{1,0:T(4,128)S(1)}, u32[]{:S(2)}, u32[]{:S(2)}) collective-permute-start(f32[4,1024]{1,0:T(4,128)S(1)} %get-tuple-element.43), channel_id=1, source_target_pairs={{0,3},{1,2},{2,1},{3,0},{4,7},{5,6},{6,5},{7,4},{8,11},{9,10},{10,... | collective-permute-start | bytes 49160 | tf_op jit(solution)/shard_map/ppermute | solution.py:57
  6.9 4.5 %collective-permute-start = (f32[3,16,1024]{2,1,0:T(8,128)S(1)}, f32[3,16,1024]{2,1,0:T(8,128)S(1)}, u32[]{:S(2)}, u32[]{:S(2)}) collective-permute-start(f32[3,16,1024]{2,1,0:T(8,128)S(1)} %get-tuple-element.35), channel_id=1, source_target_pairs={{0,4},{4,0},{8,12},{12,8},{16,20},{20,16},{24,28},{28,24},{1,5},{5... | collective-permute-start | bytes 589832 | tf_op jit(solution)/shard_map/ppermute | solution.py:45
  6.9 1.5 %collective-permute-start.1 = (f32[16,1024]{1,0:T(8,128)S(1)}, f32[16,1024]{1,0:T(8,128)S(1)}, u32[]{:S(2)}, u32[]{:S(2)}) collective-permute-start(f32[16,1024]{1,0:T(8,128)S(1)} %get-tuple-element.37), channel_id=1, source_target_pairs={{0,4},{4,0},{8,12},{12,8},{16,20},{20,16},{24,28},{28,24},{1,5},{5... | collective-permute-start | bytes 196616 | tf_op jit(solution)/shard_map/ppermute | solution.py:45
  8.5 5.2 %collective-permute-start.2 = (f32[16,1024]{1,0:T(8,128)S(1)}, f32[16,1024]{1,0:T(8,128)S(1)}, u32[]{:S(2)}, u32[]{:S(2)}) collective-permute-start(f32[16,1024]{1,0:T(8,128)S(1)} %add.24), channel_id=1, source_target_pairs={{0,20},{4,16},{8,28},{12,24},{16,4},{20,0},{24,12},{28,8},{1,21},{... | collective-permute-start | bytes 196616 | tf_op jit(solution)/shard_map/ppermute | solution.py:53
  11.4 6.0 %collective-permute-start.3 = (f32[16,1024]{1,0:T(8,128)S(1)}, f32[16,1024]{1,0:T(8,128)S(1)}, u32[]{:S(2)}, u32[]{:S(2)}) collective-permute-start(f32[16,1024]{1,0:T(8,128)S(1)} %get-tuple-element.63), channel_id=1, source_target_pairs={{0,28},{4,24},{8,20},{12,16},{16,12},{20,8},{24,4},{28,0},{1,29},{... | collective-permute-start | bytes 196616 | tf_op jit(solution)/shard_map/ppermute | solution.py:53
  13.6 6.1 %collective-permute-start.4 = (f32[16,1024]{1,0:T(8,128)S(1)}, f32[16,1024]{1,0:T(8,128)S(1)}, u32[]{:S(2)}, u32[]{:S(2)}) collective-permute-start(f32[16,1024]{1,0:T(8,128)S(1)} %get-tuple-element.62), channel_id=1, source_target_pairs={{0,12},{4,8},{8,4},{12,0},{16,28},{20,24},{24,20},{28,16},{1,13},{... | collective-permute-start | bytes 196616 | tf_op jit(solution)/shard_map/ppermute | solution.py:53
  19.9 4.3 %collective-permute-start.5 = (f32[16,1024]{1,0:T(8,128)S(1)}, f32[16,1024]{1,0:T(8,128)S(1)}, u32[]{:S(2)}, u32[]{:S(2)}) collective-permute-start(f32[16,1024]{1,0:T(8,128)S(1)} %get-tuple-element.42.refs_0_), channel_id=1, source_target_pairs={{0,2},{1,3},{2,0},{3,1},{4,6},{5,7},{6,4},{7,5},{8,10},{9,11},{10,... | collective-permute-start | bytes 196616 | tf_op jit(solution)/shard_map/ppermute | solution.py:57
  21.5 5.7 %collective-permute-start.6 = (f32[16,1024]{1,0:T(8,128)S(1)}, f32[16,1024]{1,0:T(8,128)S(1)}, u32[]{:S(2)}, u32[]{:S(2)}) collective-permute-start(f32[16,1024]{1,0:T(8,128)S(1)} %get-tuple-element.42.refs_0_), channel_id=1, source_target_pairs={{0,3},{1,2},{2,1},{3,0},{4,7},{5,6},{6,5},{7,4},{8,11},{9,10},{10,... | collective-permute-start | bytes 196616 | tf_op jit(solution)/shard_map/ppermute | solution.py:57
  22.9 4.3 %collective-permute-start.7 = (f32[16,1024]{1,0:T(8,128)S(1)}, f32[16,1024]{1,0:T(8,128)S(1)}, u32[]{:S(2)}, u32[]{:S(2)}) collective-permute-start(f32[16,1024]{1,0:T(8,128)S(1)} %get-tuple-element.42.refs_0_), channel_id=1, source_target_pairs={{0,1},{1,0},{2,3},{3,2},{4,5},{5,4},{6,7},{7,6},{8,9},{9,8},{10,11... | collective-permute-start | bytes 196616 | tf_op jit(solution)/shard_map/ppermute | solution.py:57
  23.5 14.4 %copy-start.1 = (f32[128,1024]{1,0:T(8,128)S(1)}, f32[128,1024]{1,0:T(8,128)}, u32[]{:S(2)}) copy-start(f32[128,1024]{1,0:T(8,128)} %refs_3_.3) | copy-start | bytes 1572868
  23.6 14.3 %copy-start = (f32[128,1024]{1,0:T(8,128)S(1)}, f32[128,1024]{1,0:T(8,128)}, u32[]{:S(2)}) copy-start(f32[128,1024]{1,0:T(8,128)} %refs_2_.3) | copy-start | bytes 1572868
  27.3 6.3 %collective-permute-start.13 = (f32[16,1024]{1,0:T(8,128)S(1)}, f32[16,1024]{1,0:T(8,128)S(1)}, u32[]{:S(2)}, u32[]{:S(2)}) collective-permute-start(f32[16,1024]{1,0:T(8,128)S(1)} %get-tuple-element.48.refs_0_), channel_id=1, source_target_pairs={{0,20},{4,16},{8,28},{12,24},{16,4},{20,0},{24,12},{28,8},{1,21},{... | collective-permute-start | bytes 196616 | tf_op jit(solution)/shard_map/ppermute | solution.py:53
  29.6 5.9 %collective-permute-start.14 = (f32[16,1024]{1,0:T(8,128)S(1)}, f32[16,1024]{1,0:T(8,128)S(1)}, u32[]{:S(2)}, u32[]{:S(2)}) collective-permute-start(f32[16,1024]{1,0:T(8,128)S(1)} %get-tuple-element.48.refs_0_), channel_id=1, source_target_pairs={{0,28},{4,24},{8,20},{12,16},{16,12},{20,8},{24,4},{28,0},{1,29},{... | collective-permute-start | bytes 196616 | tf_op jit(solution)/shard_map/ppermute | solution.py:53
  31.8 5.2 %collective-permute-start.11 = (f32[16,1024]{1,0:T(8,128)S(1)}, f32[16,1024]{1,0:T(8,128)S(1)}, u32[]{:S(2)}, u32[]{:S(2)}) collective-permute-start(f32[16,1024]{1,0:T(8,128)S(1)} %get-tuple-element.48.refs_0_), channel_id=1, source_target_pairs={{0,12},{4,8},{8,4},{12,0},{16,28},{20,24},{24,20},{28,16},{1,13},{... | collective-permute-start | bytes 196616 | tf_op jit(solution)/shard_map/ppermute | solution.py:53
  33.5 4.3 %collective-permute-start.17 = (f32[16,1024]{1,0:T(8,128)S(1)}, f32[16,1024]{1,0:T(8,128)S(1)}, u32[]{:S(2)}, u32[]{:S(2)}) collective-permute-start(f32[16,1024]{1,0:T(8,128)S(1)} %get-tuple-element.48.refs_0_), channel_id=1, source_target_pairs={{0,4},{4,0},{8,12},{12,8},{16,20},{20,16},{24,28},{28,24},{1,5},{5... | collective-permute-start | bytes 196616 | tf_op jit(solution)/shard_map/ppermute | solution.py:45
  33.6 5.0 %collective-permute-start.15 = (f32[16,1024]{1,0:T(8,128)S(1)}, f32[16,1024]{1,0:T(8,128)S(1)}, u32[]{:S(2)}, u32[]{:S(2)}) collective-permute-start(f32[16,1024]{1,0:T(8,128)S(1)} %collective-permute-done.13.refs_0_), channel_id=1, source_target_pairs={{0,4},{4,0},{8,12},{12,8},{16,20},{20,16},{24,28},{28,24},{1,5},{5... | collective-permute-start | bytes 196616 | tf_op jit(solution)/shard_map/ppermute | solution.py:45
  35.5 3.1 %collective-permute-start.16 = (f32[16,1024]{1,0:T(8,128)S(1)}, f32[16,1024]{1,0:T(8,128)S(1)}, u32[]{:S(2)}, u32[]{:S(2)}) collective-permute-start(f32[16,1024]{1,0:T(8,128)S(1)} %collective-permute-done.14.refs_1_), channel_id=1, source_target_pairs={{0,4},{4,0},{8,12},{12,8},{16,20},{20,16},{24,28},{28,24},{1,5},{5... | collective-permute-start | bytes 196616 | tf_op jit(solution)/shard_map/ppermute | solution.py:45
  37.0 2.5 %collective-permute-start.12 = (f32[16,1024]{1,0:T(8,128)S(1)}, f32[16,1024]{1,0:T(8,128)S(1)}, u32[]{:S(2)}, u32[]{:S(2)}) collective-permute-start(f32[16,1024]{1,0:T(8,128)S(1)} %collective-permute-done.11.refs_0_), channel_id=1, source_target_pairs={{0,4},{4,0},{8,12},{12,8},{16,20},{20,16},{24,28},{28,24},{1,5},{5... | collective-permute-start | bytes 196616 | tf_op jit(solution)/shard_map/ppermute | solution.py:45

commit v2 on v1

--- a/solution.py
+++ b/solution.py
@@ -26,14 +26,13 @@
     return index ^ step if paired(size) else lax.rem(index + (size - step), size)
 
 
-def steps_of(size):
-    if not paired(size):
-        return list(range(1, size))
-    steps, half = [], size // 2
-    while half:
-        steps += range(half, 2 * half)
-        half //= 2
-    return steps
+def farthest_first(size):
+    return list(range(size - 1, 0, -1))
+
+
+def farthest_last(size):
+    steps = farthest_first(size)
+    return steps[1:] + steps[:1]
 
 
 def packed_of(values, width):
@@ -187,26 +186,61 @@
     )(*near(*values))
 
 
-def average_kernel(groups, *refs):
-    parts, (server, result, error) = refs[:groups], refs[groups:]
-    width = server.shape[-1]
+def average_kernel(order, *refs):
+    groups = len(order)
+    parts, pieces, (result, error, server) = refs[:groups], refs[groups : 2 * groups], refs[2 * groups :]
+    piece_rows, width = pieces[0].shape
+    group = lax.axis_index("group")
+    for step, piece in zip(order, pieces):
+        server[source(group, step, groups)] = piece[...]
     total = parts[0][...]
     for other in parts[1:]:
         total = total + other[...]
-    values = total / groups + server[...]
-    packed = packed_of(values, width)
-    result[...] = packed
-    error[...] = values - packed
-
-
-def average(parts, server):
-    return pl.pallas_call(
-        functools.partial(average_kernel, len(parts)),
-        out_shape=[vmem(*server.shape)] * 2,
-        in_specs=[VMEM] * (len(parts) + 1),
+    mean = total / groups
+    for at in range(groups):
+        part = slice(at * piece_rows, (at + 1) * piece_rows)
+        values = mean[part] + server[at]
+        packed = packed_of(values, width)
+        result[part, :] = packed
+        error[at] = values - packed
+
+
+def average(parts, pieces, order):
+    groups = len(order)
+    stacked = (groups, *pieces[0].shape)
+    return pl.pallas_call(
+        functools.partial(average_kernel, order),
+        out_shape=[vmem(*parts[0].shape), vmem(*stacked)],
+        in_specs=[VMEM] * (2 * groups),
         out_specs=[VMEM] * 2,
-        compiler_params=room(),
-    )(*near(*parts, server))
+        scratch_shapes=[pltpu.VMEM(stacked, jnp.float32)],
+        compiler_params=room(parts[0].nbytes),
+    )(*near(*parts, *pieces))
+
+
+def first_kernel(chips, mine, given, variance, params, error, new_params, new_momentum, new_error, *scratch):
+    own = pltpu.make_async_copy(error.at[lax.axis_index("group")], new_error, scratch[-1])
+    own.start()
+    update_kernel([0], chips, mine, given, variance, params, new_params, new_momentum, *scratch[:-1])
+    own.wait()
+
+
+def update_first(mine, given, variance, params, error, chips):
+    shard_rows, width = mine.shape
+    buffer = (1, CORES * shard_rows, width)
+    return pl.pallas_call(
+        functools.partial(first_kernel, chips),
+        out_shape=[pltpu.HBM(params.shape, jnp.float32)] * 2 + [pltpu.HBM(error.shape[1:], jnp.float32)],
+        in_specs=[VMEM] * 5,
+        out_specs=[HBM] * 3,
+        scratch_shapes=[
+            pltpu.VMEM(buffer, jnp.float32),
+            pltpu.VMEM(buffer, jnp.float32),
+            pltpu.SemaphoreType.DMA((1, 2)),
+            pltpu.SemaphoreType.DMA,
+        ],
+        compiler_params=room(2 * CORES * mine.nbytes),
+    )(*near(mine, given, variance, params, error))
 
 
 def update_kernel(steps, chips, *refs):
@@ -263,12 +297,7 @@
     nodes = lax.axis_size("node")
     groups = lax.axis_size("group")
     chips = nodes // CORES
-    rows, width = momentum.shape
-    shard_rows = rows // nodes
-    piece_rows = group_server_error.shape[0]
-    group = lax.axis_index("group")
-    along = steps_of(chips)
-    across = steps_of(groups)
+    along, back, across = farthest_first(chips), farthest_last(chips), farthest_first(groups)
 
     small = (server_error[0], group_worker_error[0], group_server_error)
     *kept, sooner, later, error, server, worker, own_piece = head(gradient, momentum, worker_error, small, along + [0])
@@ -283,27 +312,23 @@
         got_pieces.append(send_group(own_piece, step, groups))
 
     second, error_0, error_1 = serve(parts, server, worker, nodes)
-    error_0, got_pieces = lax.optimization_barrier((error_0, got_pieces))
-    pieces = jnp.zeros((groups, piece_rows, width), jnp.float32)
-    for step, piece in zip([0] + across, [own_piece] + got_pieces):
-        pieces = lax.dynamic_update_slice_in_dim(pieces, piece[None], source(group, step, groups), 0)
     seconds = [second]
     for step in across:
         seconds.append(send_group(second, step, groups))
     new_worker_error, new_server_error, new_group_worker_error = store(error[None, None], error_0[None], error_1[None])
 
-    mine, shard_error = average(seconds, pieces.reshape(shard_rows, width))
-    new_group_server_error = lax.dynamic_slice_in_dim(shard_error, group * piece_rows, piece_rows, 0)
-
-    arrived = [mine]
-    for step in along:
-        arrived.append(send_chip(mine, step, nodes))
-    given = []
-    for step, values in zip([0] + along, arrived):
-        given.append(swap_cores(values, nodes))
-    outs = ()
-    for some in (slice(0, 1), slice(1, chips - 1), slice(chips - 1, chips)):
-        outs = update(arrived[some], given[some], variance, params, outs, ([0] + along)[some], chips)
+    mine, shard_error = average(seconds, [own_piece] + got_pieces, [0] + across)
+
+    arrived = {0: mine}
+    for step in back:
+        arrived[step] = send_chip(mine, step, nodes)
+    order = [0] + back
+    given = {}
+    for step in order:
+        given[step] = swap_cores(arrived[step], nodes)
+    *outs, new_group_server_error = update_first(mine, given[0], variance, params, shard_error, chips)
+    for some in (order[1:-1], order[-1:]):
+        outs = update([arrived[i] for i in some], [given[i] for i in some], variance, params, outs, some, chips)
     new_params, new_momentum = outs
     return (
         new_params,

time: 40.5 us -> 38.4 us (0.948)
  starting transfers between devices: 23.7 us -> 19 us
  waiting for transfers between devices: 9.86 us -> 13.2 us
  local copies, waits for them, and re-layouts: 0.71 us -> 0.02 us
    ppermute x6, starting transfers between devices: 13.4 us -> 8.67 us  [send_chip(): return lax.ppermute(values, 'node', pairs)]
    ppermute x6, waiting for transfers between devices: 5.24 us -> 9.01 us  [send_chip(): return lax.ppermute(values, 'node', pairs)]
    pallas_call x1 -> x2, Pallas kernels: 0.11 us -> 0.89 us  [the longest x1 0.76 us: update_first(): pl.pallas_call(functools.partial(first_kernel, chips), out_shape=[pltpu.H...]
    pallas_call x3 -> x2, Pallas kernels: 2.38 us -> 1.63 us  [update(): pl.pallas_call(functools.partial(update_kernel, steps, chips), out_shape=...]
    ppermute x6, waiting for transfers between devices: 3.63 us -> 2.97 us  [send_group(): lax.ppermute(values, 'group', [(i, target(i, step, groups)) for i in rang...]
    dynamic_slice x1 -> x0, local copies, waits for them, and re-layouts: 0.61 us -> none  [body(): lax.dynamic_slice_in_dim(shard_error, group * piece_rows, piece_rows, 0)]
  transfers between devices with their start and end apart: 18 -> 18, of which waited for: 7 -> 8; matrix products, arithmetic and copies ran while one was open for 2% -> 0% of each run, Pallas kernels for 7% -> 6%
where the time goes in v2:
time: 38.4 us; the launch traced here: 38.2 us
  starting transfers between devices  19 us (49%)
  waiting for transfers between devices  13.2 us (34%)
  Pallas kernels  5.28 us (14%)
  between operations  0.77 us (2%)
    ppermute x6, waiting for transfers between devices, send_chip(): return lax.ppermute(values, 'node', pairs)  9.01 us
    ppermute x6, starting transfers between devices, send_chip(): return lax.ppermute(values, 'node', pairs)  8.67 us
    ppermute x6, starting transfers between devices, send_group(): lax.ppermute(values, 'group', [(i, target(i, step, groups)) for i in rang...  8.23 us
    ppermute x6, waiting for transfers between devices, send_group(): lax.ppermute(values, 'group', [(i, target(i, step, groups)) for i in rang...  2.97 us
    ppermute x6, starting transfers between devices, swap_cores(): return lax.ppermute(values, 'node', [(i, i ^ 1) for i in range(nodes)])  2.06 us
    pallas_call x1, Pallas kernels, head(): pl.pallas_call(functools.partial(head_kernel, order), out_shape=[vmem(*sh...  1.71 us
    pallas_call x2, Pallas kernels, update(): pl.pallas_call(functools.partial(update_kernel, steps, chips), out_shape=...  1.63 us
    ppermute x6, waiting for transfers between devices, swap_cores(): return lax.ppermute(values, 'node', [(i, i ^ 1) for i in range(nodes)])  1.19 us
  transfers between devices with their start and end apart: 18, of which 8 were waited for; matrix products, arithmetic and copies ran while one was open for 0% of the time, Pallas kernels for 6%

profile of v2, /device:TPU:0, one launch (start us, length us, event | category | flops | bytes accessed | tf_op | source)
XLA Modules:
  0.0 38.2 jit_solution(827024663439443815)
XLA Ops:
  0.6 1.7 %shard_map.127 = (f32[16,1024]{1,0:T(8,128)S(1)}, f32[16,1024]{1,0:T(8,128)S(1)}, f32[16,1024]{1,0:T(8,128)S(1)}, f32[16,1024]{1,0:T(8,128)S(1)}, f32[16,1024]{1...) custom-call(bf16[1,1,128,1024]{3,2,1,0:T(8,128)(2,1)} %gradient.1, ...), custom_call_target="tpu_custom_call" | custom-call | tf_op jit(solution)/shard_map/pallas_call | solution.py:127
  2.3 0.6 %collective-permute-start = (f32[3,16,1024]{2,1,0:T(8,128)S(1)}, f32[3,16,1024]{2,1,0:T(8,128)S(1)}, u32[]{:S(2)}, u32[]{:S(2)}) collective-permute-start(f32[3,16,1024]{2,1,0:T(8,128)S(1)} %get-tuple-element.32), channel_id=1, source_target_pairs={{0,4},{4,0},{8,12},{12,8},{16,20},{20,16},{24,28},{28,24},{1,5},{5... | collective-permute-start | bytes 589832 | tf_op jit(solution)/shard_map/ppermute | solution.py:44
  2.9 0.1 collective-permute-start.1
  3.0 1.2 %collective-permute-done.1 = f32[16,1024]{1,0:T(8,128)S(1)} collective-permute-done((f32[16,1024]{1,0:T(8,128)S(1)}, f32[16,1024]{1,0:T(8,128)S(1)}, u32[]{:S(2)}, u32[]{:S(2)}) %collective-permute-start.1) | collective-permute-done | bytes 65568 | tf_op jit(solution)/shard_map/ppermute | solution.py:44
  4.2 4.8 %collective-permute-start.2 = (f32[16,1024]{1,0:T(8,128)S(1)}, f32[16,1024]{1,0:T(8,128)S(1)}, u32[]{:S(2)}, u32[]{:S(2)}) collective-permute-start(f32[16,1024]{1,0:T(8,128)S(1)} %add.9), channel_id=1, source_target_pairs={{0,28},{4,24},{8,20},{12,16},{16,12},{20,8},{24,4},{28,0},{1,29},{... | collective-permute-start | bytes 196616 | tf_op jit(solution)/shard_map/ppermute | solution.py:52
  8.9 0.0 collective-permute-done
  9.0 0.1 collective-permute-start.3
  9.0 0.5 %collective-permute-start.4 = (f32[16,1024]{1,0:T(8,128)S(1)}, f32[16,1024]{1,0:T(8,128)S(1)}, u32[]{:S(2)}, u32[]{:S(2)}) collective-permute-start(f32[16,1024]{1,0:T(8,128)S(1)} %get-tuple-element.56), channel_id=1, source_target_pairs={{0,12},{4,8},{8,4},{12,0},{16,28},{20,24},{24,20},{28,16},{1,13},{... | collective-permute-start | bytes 196616 | tf_op jit(solution)/shard_map/ppermute | solution.py:52
  9.5 2.0 %collective-permute-done.2.refs_2_ = f32[16,1024]{1,0:T(8,128)S(1)} collective-permute-done((f32[16,1024]{1,0:T(8,128)S(1)}, f32[16,1024]{1,0:T(8,128)S(1)}, u32[]{:S(2)}, u32[]{:S(2)}) %collective-permute-start.2) | collective-permute-done | bytes 65568 | tf_op jit(solution)/shard_map/ppermute | solution.py:52
  11.5 3.2 %collective-permute-done.3.refs_3_ = f32[16,1024]{1,0:T(8,128)S(1)} collective-permute-done((f32[16,1024]{1,0:T(8,128)S(1)}, f32[16,1024]{1,0:T(8,128)S(1)}, u32[]{:S(2)}, u32[]{:S(2)}) %collective-permute-start.3) | collective-permute-done | bytes 65568 | tf_op jit(solution)/shard_map/ppermute | solution.py:52
  14.7 0.0 collective-permute-done.4.refs_4_
  14.7 0.0 copy-start.1
  14.7 0.2 shard_map.128
  14.9 0.0 copy-start
  14.9 2.5 %collective-permute-start.5 = (f32[16,1024]{1,0:T(8,128)S(1)}, f32[16,1024]{1,0:T(8,128)S(1)}, u32[]{:S(2)}, u32[]{:S(2)}) collective-permute-start(f32[16,1024]{1,0:T(8,128)S(1)} %get-tuple-element.39.refs_0_), channel_id=1, source_target_pairs={{0,3},{1,2},{2,1},{3,0},{4,7},{5,6},{6,5},{7,4},{8,11},{9,10},{10,... | collective-permute-start | bytes 196616 | tf_op jit(solution)/shard_map/ppermute | solution.py:56
  17.4 0.5 %collective-permute-start.6 = (f32[16,1024]{1,0:T(8,128)S(1)}, f32[16,1024]{1,0:T(8,128)S(1)}, u32[]{:S(2)}, u32[]{:S(2)}) collective-permute-start(f32[16,1024]{1,0:T(8,128)S(1)} %get-tuple-element.39.refs_0_), channel_id=1, source_target_pairs={{0,2},{1,3},{2,0},{3,1},{4,6},{5,7},{6,4},{7,5},{8,10},{9,11},{10,... | collective-permute-start | bytes 196616 | tf_op jit(solution)/shard_map/ppermute | solution.py:56
  18.0 0.5 %collective-permute-start.7 = (f32[16,1024]{1,0:T(8,128)S(1)}, f32[16,1024]{1,0:T(8,128)S(1)}, u32[]{:S(2)}, u32[]{:S(2)}) collective-permute-start(f32[16,1024]{1,0:T(8,128)S(1)} %get-tuple-element.39.refs_0_), channel_id=1, source_target_pairs={{0,1},{1,0},{2,3},{3,2},{4,5},{5,4},{6,7},{7,6},{8,9},{9,8},{10,11... | collective-permute-start | bytes 196616 | tf_op jit(solution)/shard_map/ppermute | solution.py:56
  18.5 1.5 %collective-permute-start.10 = (f32[4,1024]{1,0:T(4,128)S(1)}, f32[4,1024]{1,0:T(4,128)S(1)}, u32[]{:S(2)}, u32[]{:S(2)}) collective-permute-start(f32[4,1024]{1,0:T(4,128)S(1)} %get-tuple-element.40.refs_4_), channel_id=1, source_target_pairs={{0,1},{1,0},{2,3},{3,2},{4,5},{5,4},{6,7},{7,6},{8,9},{9,8},{10,11... | collective-permute-start | bytes 49160 | tf_op jit(solution)/shard_map/ppermute | solution.py:56
  20.0 1.5 %collective-permute-start.8 = (f32[4,1024]{1,0:T(4,128)S(1)}, f32[4,1024]{1,0:T(4,128)S(1)}, u32[]{:S(2)}, u32[]{:S(2)}) collective-permute-start(f32[4,1024]{1,0:T(4,128)S(1)} %get-tuple-element.40.refs_4_), channel_id=1, source_target_pairs={{0,3},{1,2},{2,1},{3,0},{4,7},{5,6},{6,5},{7,4},{8,11},{9,10},{10,... | collective-permute-start | bytes 49160 | tf_op jit(solution)/shard_map/ppermute | solution.py:56
  21.5 0.9 %collective-permute-done.10.refs_7_ = f32[4,1024]{1,0:T(4,128)S(1)} collective-permute-done((f32[4,1024]{1,0:T(4,128)S(1)}, f32[4,1024]{1,0:T(4,128)S(1)}, u32[]{:S(2)}, u32[]{:S(2)}) %collective-permute-start.10) | collective-permute-done | bytes 16416 | tf_op jit(solution)/shard_map/ppermute | solution.py:56
  22.4 1.7 %collective-permute-start.9 = (f32[4,1024]{1,0:T(4,128)S(1)}, f32[4,1024]{1,0:T(4,128)S(1)}, u32[]{:S(2)}, u32[]{:S(2)}) collective-permute-start(f32[4,1024]{1,0:T(4,128)S(1)} %get-tuple-element.40.refs_4_), channel_id=1, source_target_pairs={{0,2},{1,3},{2,0},{3,1},{4,6},{5,7},{6,4},{7,5},{8,10},{9,11},{10,... | collective-permute-start | bytes 49160 | tf_op jit(solution)/shard_map/ppermute | solution.py:56
  24.1 0.5 %collective-permute-done.8.refs_5_ = f32[4,1024]{1,0:T(4,128)S(1)} collective-permute-done((f32[4,1024]{1,0:T(4,128)S(1)}, f32[4,1024]{1,0:T(4,128)S(1)}, u32[]{:S(2)}, u32[]{:S(2)}) %collective-permute-start.8) | collective-permute-done | bytes 16416 | tf_op jit(solution)/shard_map/ppermute | solution.py:56
  24.6 1.5 %collective-permute-done.9.refs_6_ = f32[4,1024]{1,0:T(4,128)S(1)} collective-permute-done((f32[4,1024]{1,0:T(4,128)S(1)}, f32[4,1024]{1,0:T(4,128)S(1)}, u32[]{:S(2)}, u32[]{:S(2)}) %collective-permute-start.9) | collective-permute-done | bytes 16416 | tf_op jit(solution)/shard_map/ppermute | solution.py:56
  26.1 0.0 collective-permute-done.5.refs_1_
  26.1 0.0 collective-permute-done.6.refs_2_
  26.1 0.0 collective-permute-done.7.refs_3_
  26.1 0.1 shard_map.129
  26.3 0.1 collective-permute-start.13
  26.4 2.9 %collective-permute-start.14 = (f32[16,1024]{1,0:T(8,128)S(1)}, f32[16,1024]{1,0:T(8,128)S(1)}, u32[]{:S(2)}, u32[]{:S(2)}) collective-permute-start(f32[16,1024]{1,0:T(8,128)S(1)} %get-tuple-element.41.mine), channel_id=1, source_target_pairs={{0,12},{4,8},{8,4},{12,0},{16,28},{20,24},{24,20},{28,16},{1,13},{... | collective-permute-start | bytes 196616 | tf_op jit(solution)/shard_map/ppermute | solution.py:52
  29.3 0.4 %collective-permute-start.11 = (f32[16,1024]{1,0:T(8,128)S(1)}, f32[16,1024]{1,0:T(8,128)S(1)}, u32[]{:S(2)}, u32[]{:S(2)}) collective-permute-start(f32[16,1024]{1,0:T(8,128)S(1)} %get-tuple-element.41.mine), channel_id=1, source_target_pairs={{0,28},{4,24},{8,20},{12,16},{16,12},{20,8},{24,4},{28,0},{1,29},{... | collective-permute-start | bytes 196616 | tf_op jit(solution)/shard_map/ppermute | solution.py:52
  29.7 0.9 %collective-permute-start.17 = (f32[16,1024]{1,0:T(8,128)S(1)}, f32[16,1024]{1,0:T(8,128)S(1)}, u32[]{:S(2)}, u32[]{:S(2)}) collective-permute-start(f32[16,1024]{1,0:T(8,128)S(1)} %get-tuple-element.41.mine), channel_id=1, source_target_pairs={{0,4},{4,0},{8,12},{12,8},{16,20},{20,16},{24,28},{28,24},{1,5},{5... | collective-permute-start | bytes 196616 | tf_op jit(solution)/shard_map/ppermute | solution.py:44
  30.6 1.8 %collective-permute-done.13.refs_0_ = f32[16,1024]{1,0:T(8,128)S(1)} collective-permute-done((f32[16,1024]{1,0:T(8,128)S(1)}, f32[16,1024]{1,0:T(8,128)S(1)}, u32[]{:S(2)}, u32[]{:S(2)}) %collective-permute-start.13) | collective-permute-done | bytes 65568 | tf_op jit(solution)/shard_map/ppermute | solution.py:52
  32.4 0.0 collective-permute-start.15
  32.4 0.0 collective-permute-done.14.refs_1_
  32.4 0.5 %collective-permute-start.16 = (f32[16,1024]{1,0:T(8,128)S(1)}, f32[16,1024]{1,0:T(8,128)S(1)}, u32[]{:S(2)}, u32[]{:S(2)}) collective-permute-start(f32[16,1024]{1,0:T(8,128)S(1)} %collective-permute-done.14.refs_1_), channel_id=1, source_target_pairs={{0,4},{4,0},{8,12},{12,8},{16,20},{20,16},{24,28},{28,24},{1,5},{5... | collective-permute-start | bytes 196616 | tf_op jit(solution)/shard_map/ppermute | solution.py:44
  32.9 2.0 %collective-permute-done.11.refs_0_ = f32[16,1024]{1,0:T(8,128)S(1)} collective-permute-done((f32[16,1024]{1,0:T(8,128)S(1)}, f32[16,1024]{1,0:T(8,128)S(1)}, u32[]{:S(2)}, u32[]{:S(2)}) %collective-permute-start.11) | collective-permute-done | bytes 65568 | tf_op jit(solution)/shard_map/ppermute | solution.py:52
  34.9 0.0 collective-permute-start.12
  34.9 0.8 %shard_map.133 = (f32[1,1,128,1024]{3,2,1,0:T(8,128)}, f32[1,16,1024]{2,1,0:T(8,128)}, f32[1,16,1024]{2,1,0:T(8,128)}) custom-call(f32[1,1,128,1024]{3,2,1,0:T(8,128)S(1)} %bitcast.15, f32[1,16,1024]{2,1,0:T(8,128)S(1)} %bitcast.16, f32[1,16,1024]{2,1,0:T(8,128)S(1)} %bitcast.17), custom_call_target="tpu_custom_call" | custom-call | tf_op jit(solution)/shard_map/pallas_call | solution.py:179
  35.7 0.0 collective-permute-done.17.given
  35.8 0.0 copy-done.1
  35.8 0.0 copy-done
  35.8 0.8 %shard_map.130 = (f32[128,1024]{1,0:T(8,128)}, f32[128,1024]{1,0:T(8,128)}, f32[4,1024]{1,0:T(4,128)}) custom-call(f32[16,1024]{1,0:T(8,128)S(1)} %get-tuple-element.41.mine, f32[16,1024]{1,0:T(8,128)S(1)} %collective-permute-done.17.given, f32[128,1024]{1,0:T(8,128)S(1)} %copy-done, f32[128,1024]{1,0:T(8,128)S(1)} %copy-done.1, ...), custom_call_target="tpu_custom_call" | custom-call | tf_op jit(solution)/shard_map/pallas_call | solution.py:231
  36.5 0.0 collective-permute-done.15.refs_2_
  36.6 0.0 collective-permute-done.16.refs_3_
  36.6 0.9 %shard_map.131 = (f32[128,1024]{1,0:T(8,128)}, f32[128,1024]{1,0:T(8,128)}) custom-call(f32[16,1024]{1,0:T(8,128)S(1)} %collective-permute-done.13.refs_0_, f32[16,1024]{1,0:T(8,128)S(1)} %collective-permute-done.14.refs_1_, f32[16,1024]{1,0:T(8,128)S(1)} %collective-permute-done.15.refs_2_, ...), custom_call_target="tpu_custom_call", output_to_operand_aliasing={{0}: (6, {}), {1}: (7, {})} | custom-call | tf_op jit(solution)/shard_map/pallas_call | solution.py:272
  37.4 0.0 collective-permute-done.12.refs_1_
  37.5 0.8 %shard_map.132 = (f32[128,1024]{1,0:T(8,128)}, f32[128,1024]{1,0:T(8,128)}) custom-call(f32[16,1024]{1,0:T(8,128)S(1)} %collective-permute-done.11.refs_0_, f32[16,1024]{1,0:T(8,128)S(1)} %collective-permute-done.12.refs_1_, f32[128,1024]{1,0:T(8,128)S(1)} %copy-done, f32[128,1024]{1,0:T(8,128)S(1)} %copy-done.1, ...), custom_call_target="tpu_custom_call", output_to_operand_aliasing={{0}: (4, {}), {1}: (5, {})} | custom-call | tf_op jit(solution)/shard_map/pallas_call | solution.py:272
  (3 shorter events, 0.0 us)
Async XLA Ops:
  2.3 6.6 %collective-permute-start = (f32[3,16,1024]{2,1,0:T(8,128)S(1)}, f32[3,16,1024]{2,1,0:T(8,128)S(1)}, u32[]{:S(2)}, u32[]{:S(2)}) collective-permute-start(f32[3,16,1024]{2,1,0:T(8,128)S(1)} %get-tuple-element.32), channel_id=1, source_target_pairs={{0,4},{4,0},{8,12},{12,8},{16,20},{20,16},{24,28},{28,24},{1,5},{5... | collective-permute-start | bytes 589832 | tf_op jit(solution)/shard_map/ppermute | solution.py:44
  2.9 1.3 %collective-permute-start.1 = (f32[16,1024]{1,0:T(8,128)S(1)}, f32[16,1024]{1,0:T(8,128)S(1)}, u32[]{:S(2)}, u32[]{:S(2)}) collective-permute-start(f32[16,1024]{1,0:T(8,128)S(1)} %get-tuple-element.34), channel_id=1, source_target_pairs={{0,4},{4,0},{8,12},{12,8},{16,20},{20,16},{24,28},{28,24},{1,5},{5... | collective-permute-start | bytes 196616 | tf_op jit(solution)/shard_map/ppermute | solution.py:44
  4.2 7.3 %collective-permute-start.2 = (f32[16,1024]{1,0:T(8,128)S(1)}, f32[16,1024]{1,0:T(8,128)S(1)}, u32[]{:S(2)}, u32[]{:S(2)}) collective-permute-start(f32[16,1024]{1,0:T(8,128)S(1)} %add.9), channel_id=1, source_target_pairs={{0,28},{4,24},{8,20},{12,16},{16,12},{20,8},{24,4},{28,0},{1,29},{... | collective-permute-start | bytes 196616 | tf_op jit(solution)/shard_map/ppermute | solution.py:52
  9.0 5.7 %collective-permute-start.3 = (f32[16,1024]{1,0:T(8,128)S(1)}, f32[16,1024]{1,0:T(8,128)S(1)}, u32[]{:S(2)}, u32[]{:S(2)}) collective-permute-start(f32[16,1024]{1,0:T(8,128)S(1)} %get-tuple-element.57), channel_id=1, source_target_pairs={{0,20},{4,16},{8,28},{12,24},{16,4},{20,0},{24,12},{28,8},{1,21},{... | collective-permute-start | bytes 196616 | tf_op jit(solution)/shard_map/ppermute | solution.py:52
  9.0 5.7 %collective-permute-start.4 = (f32[16,1024]{1,0:T(8,128)S(1)}, f32[16,1024]{1,0:T(8,128)S(1)}, u32[]{:S(2)}, u32[]{:S(2)}) collective-permute-start(f32[16,1024]{1,0:T(8,128)S(1)} %get-tuple-element.56), channel_id=1, source_target_pairs={{0,12},{4,8},{8,4},{12,0},{16,28},{20,24},{24,20},{28,16},{1,13},{... | collective-permute-start | bytes 196616 | tf_op jit(solution)/shard_map/ppermute | solution.py:52
  14.7 21.0 %copy-start.1 = (f32[128,1024]{1,0:T(8,128)S(1)}, f32[128,1024]{1,0:T(8,128)}, u32[]{:S(2)}) copy-start(f32[128,1024]{1,0:T(8,128)} %refs_3_.1) | copy-start | bytes 1572868
  14.9 20.8 %copy-start = (f32[128,1024]{1,0:T(8,128)S(1)}, f32[128,1024]{1,0:T(8,128)}, u32[]{:S(2)}) copy-start(f32[128,1024]{1,0:T(8,128)} %refs_2_.1) | copy-start | bytes 1572868
  14.9 11.2 %collective-permute-start.5 = (f32[16,1024]{1,0:T(8,128)S(1)}, f32[16,1024]{1,0:T(8,128)S(1)}, u32[]{:S(2)}, u32[]{:S(2)}) collective-permute-start(f32[16,1024]{1,0:T(8,128)S(1)} %get-tuple-element.39.refs_0_), channel_id=1, source_target_pairs={{0,3},{1,2},{2,1},{3,0},{4,7},{5,6},{6,5},{7,4},{8,11},{9,10},{10,... | collective-permute-start | bytes 196616 | tf_op jit(solution)/shard_map/ppermute | solution.py:56
  17.4 8.7 %collective-permute-start.6 = (f32[16,1024]{1,0:T(8,128)S(1)}, f32[16,1024]{1,0:T(8,128)S(1)}, u32[]{:S(2)}, u32[]{:S(2)}) collective-permute-start(f32[16,1024]{1,0:T(8,128)S(1)} %get-tuple-element.39.refs_0_), channel_id=1, source_target_pairs={{0,2},{1,3},{2,0},{3,1},{4,6},{5,7},{6,4},{7,5},{8,10},{9,11},{10,... | collective-permute-start | bytes 196616 | tf_op jit(solution)/shard_map/ppermute | solution.py:56
  18.0 8.2 %collective-permute-start.7 = (f32[16,1024]{1,0:T(8,128)S(1)}, f32[16,1024]{1,0:T(8,128)S(1)}, u32[]{:S(2)}, u32[]{:S(2)}) collective-permute-start(f32[16,1024]{1,0:T(8,128)S(1)} %get-tuple-element.39.refs_0_), channel_id=1, source_target_pairs={{0,1},{1,0},{2,3},{3,2},{4,5},{5,4},{6,7},{7,6},{8,9},{9,8},{10,11... | collective-permute-start | bytes 196616 | tf_op jit(solution)/shard_map/ppermute | solution.py:56
  18.5 3.9 %collective-permute-start.10 = (f32[4,1024]{1,0:T(4,128)S(1)}, f32[4,1024]{1,0:T(4,128)S(1)}, u32[]{:S(2)}, u32[]{:S(2)}) collective-permute-start(f32[4,1024]{1,0:T(4,128)S(1)} %get-tuple-element.40.refs_4_), channel_id=1, source_target_pairs={{0,1},{1,0},{2,3},{3,2},{4,5},{5,4},{6,7},{7,6},{8,9},{9,8},{10,11... | collective-permute-start | bytes 49160 | tf_op jit(solution)/shard_map/ppermute | solution.py:56
  20.0 4.6 %collective-permute-start.8 = (f32[4,1024]{1,0:T(4,128)S(1)}, f32[4,1024]{1,0:T(4,128)S(1)}, u32[]{:S(2)}, u32[]{:S(2)}) collective-permute-start(f32[4,1024]{1,0:T(4,128)S(1)} %get-tuple-element.40.refs_4_), channel_id=1, source_target_pairs={{0,3},{1,2},{2,1},{3,0},{4,7},{5,6},{6,5},{7,4},{8,11},{9,10},{10,... | collective-permute-start | bytes 49160 | tf_op jit(solution)/shard_map/ppermute | solution.py:56
  22.4 3.7 %collective-permute-start.9 = (f32[4,1024]{1,0:T(4,128)S(1)}, f32[4,1024]{1,0:T(4,128)S(1)}, u32[]{:S(2)}, u32[]{:S(2)}) collective-permute-start(f32[4,1024]{1,0:T(4,128)S(1)} %get-tuple-element.40.refs_4_), channel_id=1, source_target_pairs={{0,2},{1,3},{2,0},{3,1},{4,6},{5,7},{6,4},{7,5},{8,10},{9,11},{10,... | collective-permute-start | bytes 49160 | tf_op jit(solution)/shard_map/ppermute | solution.py:56
  26.3 6.1 %collective-permute-start.13 = (f32[16,1024]{1,0:T(8,128)S(1)}, f32[16,1024]{1,0:T(8,128)S(1)}, u32[]{:S(2)}, u32[]{:S(2)}) collective-permute-start(f32[16,1024]{1,0:T(8,128)S(1)} %get-tuple-element.41.mine), channel_id=1, source_target_pairs={{0,20},{4,16},{8,28},{12,24},{16,4},{20,0},{24,12},{28,8},{1,21},{... | collective-permute-start | bytes 196616 | tf_op jit(solution)/shard_map/ppermute | solution.py:52
  26.4 6.1 %collective-permute-start.14 = (f32[16,1024]{1,0:T(8,128)S(1)}, f32[16,1024]{1,0:T(8,128)S(1)}, u32[]{:S(2)}, u32[]{:S(2)}) collective-permute-start(f32[16,1024]{1,0:T(8,128)S(1)} %get-tuple-element.41.mine), channel_id=1, source_target_pairs={{0,12},{4,8},{8,4},{12,0},{16,28},{20,24},{24,20},{28,16},{1,13},{... | collective-permute-start | bytes 196616 | tf_op jit(solution)/shard_map/ppermute | solution.py:52
  29.3 5.6 %collective-permute-start.11 = (f32[16,1024]{1,0:T(8,128)S(1)}, f32[16,1024]{1,0:T(8,128)S(1)}, u32[]{:S(2)}, u32[]{:S(2)}) collective-permute-start(f32[16,1024]{1,0:T(8,128)S(1)} %get-tuple-element.41.mine), channel_id=1, source_target_pairs={{0,28},{4,24},{8,20},{12,16},{16,12},{20,8},{24,4},{28,0},{1,29},{... | collective-permute-start | bytes 196616 | tf_op jit(solution)/shard_map/ppermute | solution.py:52
  29.7 6.1 %collective-permute-start.17 = (f32[16,1024]{1,0:T(8,128)S(1)}, f32[16,1024]{1,0:T(8,128)S(1)}, u32[]{:S(2)}, u32[]{:S(2)}) collective-permute-start(f32[16,1024]{1,0:T(8,128)S(1)} %get-tuple-element.41.mine), channel_id=1, source_target_pairs={{0,4},{4,0},{8,12},{12,8},{16,20},{20,16},{24,28},{28,24},{1,5},{5... | collective-permute-start | bytes 196616 | tf_op jit(solution)/shard_map/ppermute | solution.py:44
  32.4 4.1 %collective-permute-start.15 = (f32[16,1024]{1,0:T(8,128)S(1)}, f32[16,1024]{1,0:T(8,128)S(1)}, u32[]{:S(2)}, u32[]{:S(2)}) collective-permute-start(f32[16,1024]{1,0:T(8,128)S(1)} %collective-permute-done.13.refs_0_), channel_id=1, source_target_pairs={{0,4},{4,0},{8,12},{12,8},{16,20},{20,16},{24,28},{28,24},{1,5},{5... | collective-permute-start | bytes 196616 | tf_op jit(solution)/shard_map/ppermute | solution.py:44
  32.4 4.1 %collective-permute-start.16 = (f32[16,1024]{1,0:T(8,128)S(1)}, f32[16,1024]{1,0:T(8,128)S(1)}, u32[]{:S(2)}, u32[]{:S(2)}) collective-permute-start(f32[16,1024]{1,0:T(8,128)S(1)} %collective-permute-done.14.refs_1_), channel_id=1, source_target_pairs={{0,4},{4,0},{8,12},{12,8},{16,20},{20,16},{24,28},{28,24},{1,5},{5... | collective-permute-start | bytes 196616 | tf_op jit(solution)/shard_map/ppermute | solution.py:44
  34.9 2.6 %collective-permute-start.12 = (f32[16,1024]{1,0:T(8,128)S(1)}, f32[16,1024]{1,0:T(8,128)S(1)}, u32[]{:S(2)}, u32[]{:S(2)}) collective-permute-start(f32[16,1024]{1,0:T(8,128)S(1)} %collective-permute-done.11.refs_0_), channel_id=1, source_target_pairs={{0,4},{4,0},{8,12},{12,8},{16,20},{20,16},{24,28},{28,24},{1,5},{5... | collective-permute-start | bytes 196616 | tf_op jit(solution)/shard_map/ppermute | solution.py:44

commit v3 on v2

--- a/solution.py
+++ b/solution.py
@@ -35,6 +35,10 @@
     return steps[1:] + steps[:1]
 
 
+def crossed_back(step):
+    return step > 0 and step % 2 == 0
+
+
 def packed_of(values, width):
     scale = jnp.sum(jnp.abs(values), axis=-1, keepdims=True) / width
     return jnp.where(values > 0, scale, jnp.where(values < 0, -scale, jnp.zeros_like(values)))
@@ -44,10 +48,12 @@
     return lax.ppermute(values, "node", [(i, i ^ 1) for i in range(nodes)])
 
 
-def send_chip(values, step, nodes):
+def send_chip(values, step, nodes, crossed):
     chips = nodes // CORES
     pairs = [
-        (CORES * i + core, CORES * target(i, step, chips) + 1 - core) for i in range(chips) for core in range(CORES)
+        (CORES * i + core, CORES * target(i, step, chips) + (1 - core if crossed else core))
+        for i in range(chips)
+        for core in range(CORES)
     ]
     return lax.ppermute(values, "node", pairs)
 
@@ -77,35 +83,35 @@
     return node // CORES, lax.rem(node, CORES)
 
 
-def head_kernel(order, gradient, momentum, worker_error, *rest):
+def head_kernel(order, joined, gradient, momentum, worker_error, *rest):
     chips = len(order)
-    small, rest = rest[:3], rest[3:]
-    kept, (sooner, later, error, *near_small, g_buf, m_buf, w_buf, sems, small_sems) = rest[:chips], rest[chips:]
+    kept, (sooner, later, error, g_buf, m_buf, w_buf, sems) = rest[:chips], rest[chips:]
     rows, width = momentum.shape
     chip_rows = rows // chips
     shard_rows = chip_rows // CORES
+    block_rows = joined * chip_rows
     chip, core = place_of()
-    copies = []
-    for at, step in enumerate(order):
-        where = target(chip, step, chips)
-        part = pl.ds(pl.multiple_of(where * chip_rows, chip_rows), chip_rows)
+    blocks = []
+    for at in range(0, chips, joined):
+        block = target(chip, order[at], chips) // joined
+        part = pl.ds(pl.multiple_of(block * block_rows, block_rows), block_rows)
         pairs = ((gradient.at[0, 0], g_buf), (momentum, m_buf), (worker_error.at[0, 0], w_buf))
         three = [
-            pltpu.make_async_copy(src.at[part], dst.at[at], sems.at[at, kind]) for kind, (src, dst) in enumerate(pairs)
+            pltpu.make_async_copy(src.at[part], dst.at[part], sems.at[at // joined, kind])
+            for kind, (src, dst) in enumerate(pairs)
         ]
         for copy in three:
             copy.start()
-        copies.append((where, three))
-    brought = [pltpu.make_async_copy(src, dst, small_sems.at[i]) for i, (src, dst) in enumerate(zip(small, near_small))]
-    for copy in brought:
-        copy.start()
-    for at, (where, three) in enumerate(copies):
-        for copy in three:
-            copy.wait()
-        mine = core if order[at] == 0 else 1 - core
+        blocks.append(three)
+    for at, step in enumerate(order):
+        if at % joined == 0:
+            for copy in blocks[at // joined]:
+                copy.wait()
+        where = target(chip, step, chips)
+        mine = 1 - core if step else core
         for side, half in enumerate((mine, 1 - mine)):
-            some = pl.ds(pl.multiple_of(half * shard_rows, shard_rows), shard_rows)
-            local = 0.9 * m_buf[at, some] + 0.1 * g_buf[at, some].astype(jnp.float32) + w_buf[at, some]
+            some = pl.ds(pl.multiple_of(where * chip_rows + half * shard_rows, shard_rows), shard_rows)
+            local = 0.9 * m_buf[some, :] + 0.1 * g_buf[some, :].astype(jnp.float32) + w_buf[some, :]
             first = packed_of(local, width)
             if side == 0:
                 kept[at][...] = first
@@ -113,36 +119,33 @@
                 sooner[...] = first
             else:
                 later[at - 1] = first
-            start = pl.multiple_of(where * chip_rows + half * shard_rows, shard_rows)
-            error[pl.ds(start, shard_rows), :] = local - first
-    for copy in brought:
-        copy.wait()
-
-
-def head(gradient, momentum, worker_error, small, order):
+            error[some, :] = local - first
+
+
+def head(gradient, momentum, worker_error, order):
     rows, width = momentum.shape
     chips = len(order)
-    chip_rows = rows // chips
-    shard = (chip_rows // CORES, width)
-    return pl.pallas_call(
-        functools.partial(head_kernel, order),
-        out_shape=[vmem(*shard)] * (chips + 1) + [vmem(chips - 1, *shard), vmem(rows, width)] + [vmem(*x.shape) for x in small],
-        in_specs=[HBM] * 6,
-        out_specs=[VMEM] * (chips + 6),
+    shard = (rows // chips // CORES, width)
+    joined = 2 if paired(chips) and chips % 2 == 0 else 1
+    return pl.pallas_call(
+        functools.partial(head_kernel, order, joined),
+        out_shape=[vmem(*shard)] * (chips + 1) + [vmem(chips - 1, *shard), vmem(rows, width)],
+        in_specs=[HBM] * 3,
+        out_specs=[VMEM] * (chips + 3),
         scratch_shapes=[
-            pltpu.VMEM((chips, chip_rows, width), gradient.dtype),
-            pltpu.VMEM((chips, chip_rows, width), jnp.float32),
-            pltpu.VMEM((chips, chip_rows, width), jnp.float32),
-            pltpu.SemaphoreType.DMA((chips, 3)),
-            pltpu.SemaphoreType.DMA((3,)),
+            pltpu.VMEM((rows, width), gradient.dtype),
+            pltpu.VMEM((rows, width), jnp.float32),
+            pltpu.VMEM((rows, width), jnp.float32),
+            pltpu.SemaphoreType.DMA((chips // joined, 3)),
         ],
         compiler_params=room(gradient.nbytes, momentum.nbytes, worker_error.nbytes),
-    )(*far(gradient, momentum, worker_error, *small))
-
-
-def server_kernel(nodes, count, *refs):
-    parts, (server, worker, second, error_0, error_1) = refs[:count], refs[count:]
+    )(*far(gradient, momentum, worker_error))
+
+
+def server_kernel(nodes, groups, count, *refs):
+    parts, (server, worker, piece, second, error_0, error_1) = refs[:count], refs[count:]
     width = server.shape[-1]
+    piece_rows = piece.shape[0]
     total = parts[0][...]
     for other in parts[1:]:
         total = total + other[...]
@@ -151,18 +154,21 @@
     error_0[...] = values - group_q
     values = group_q + worker[...]
     result = packed_of(values, width)
-    second[...] = result
     error_1[...] = values - result
-
-
-def serve(parts, server, worker, nodes):
-    return pl.pallas_call(
-        functools.partial(server_kernel, nodes, len(parts)),
+    group = lax.axis_index("group")
+    for at in range(groups):
+        part = slice(at * piece_rows, (at + 1) * piece_rows)
+        second[part, :] = result[part] + jnp.where(group == at, groups * piece[...], jnp.zeros_like(piece))
+
+
+def serve(parts, server, worker, piece, nodes, groups):
+    return pl.pallas_call(
+        functools.partial(server_kernel, nodes, groups, len(parts)),
         out_shape=[vmem(*server.shape)] * 3,
-        in_specs=[VMEM] * (len(parts) + 2),
+        in_specs=[VMEM] * (len(parts) + 3),
         out_specs=[VMEM] * 3,
         compiler_params=room(),
-    )(*near(*parts, server, worker))
+    )(*near(*parts, server, worker, piece))
 
 
 def store_kernel(count, *refs):
@@ -186,36 +192,30 @@
     )(*near(*values))
 
 
-def average_kernel(order, *refs):
-    groups = len(order)
-    parts, pieces, (result, error, server) = refs[:groups], refs[groups : 2 * groups], refs[2 * groups :]
-    piece_rows, width = pieces[0].shape
-    group = lax.axis_index("group")
-    for step, piece in zip(order, pieces):
-        server[source(group, step, groups)] = piece[...]
+def average_kernel(groups, *refs):
+    parts, (result, error) = refs[:groups], refs[groups:]
+    piece_rows, width = error.shape[1:]
     total = parts[0][...]
     for other in parts[1:]:
         total = total + other[...]
-    mean = total / groups
+    values = total / groups
+    packed = packed_of(values, width)
+    result[...] = packed
     for at in range(groups):
         part = slice(at * piece_rows, (at + 1) * piece_rows)
-        values = mean[part] + server[at]
-        packed = packed_of(values, width)
-        result[part, :] = packed
-        error[at] = values - packed
-
-
-def average(parts, pieces, order):
-    groups = len(order)
-    stacked = (groups, *pieces[0].shape)
-    return pl.pallas_call(
-        functools.partial(average_kernel, order),
-        out_shape=[vmem(*parts[0].shape), vmem(*stacked)],
-        in_specs=[VMEM] * (2 * groups),
+        error[at] = values[part] - packed[part]
+
+
+def average(parts):
+    groups = len(parts)
+    rows, width = parts[0].shape
+    return pl.pallas_call(
+        functools.partial(average_kernel, groups),
+        out_shape=[vmem(rows, width), vmem(groups, rows // groups, width)],
+        in_specs=[VMEM] * groups,
         out_specs=[VMEM] * 2,
-        scratch_shapes=[pltpu.VMEM(stacked, jnp.float32)],
-        compiler_params=room(parts[0].nbytes),
-    )(*near(*parts, *pieces))
+        compiler_params=room(),
+    )(*near(*parts))
 
 
 def first_kernel(chips, mine, given, variance, params, error, new_params, new_momentum, new_error, *scratch):
@@ -253,7 +253,7 @@
     copies = []
     for at, step in enumerate(steps):
         part = pl.ds(pl.multiple_of(source(chip, step, chips) * chip_rows, chip_rows), chip_rows)
-        half = core if step == 0 else 1 - core
+        half = 1 - core if crossed_back(step) else core
         for values, side in ((mine[at], half), (given[at], 1 - half)):
             m_buf[at, pl.ds(pl.multiple_of(side * shard_rows, shard_rows), shard_rows), :] = values[...]
         copies.append(pltpu.make_async_copy(m_buf.at[at], new_momentum.at[part], sems.at[at, 0]))
@@ -299,29 +299,24 @@
     chips = nodes // CORES
     along, back, across = farthest_first(chips), farthest_last(chips), farthest_first(groups)
 
-    small = (server_error[0], group_worker_error[0], group_server_error)
-    *kept, sooner, later, error, server, worker, own_piece = head(gradient, momentum, worker_error, small, along + [0])
+    *kept, sooner, later, error = head(gradient, momentum, worker_error, along + [0])
     got = [swap_cores(sooner, nodes)]
     got += list(swap_cores(later, nodes))
     parts = [kept[-1], got[-1]]
     for at, step in enumerate(along):
-        parts.append(send_chip(kept[at] + got[at], step, nodes))
-
-    got_pieces = []
-    for step in across:
-        got_pieces.append(send_group(own_piece, step, groups))
-
-    second, error_0, error_1 = serve(parts, server, worker, nodes)
+        parts.append(send_chip(kept[at] + got[at], step, nodes, True))
+
+    second, error_0, error_1 = serve(parts, server_error[0], group_worker_error[0], group_server_error, nodes, groups)
     seconds = [second]
     for step in across:
         seconds.append(send_group(second, step, groups))
     new_worker_error, new_server_error, new_group_worker_error = store(error[None, None], error_0[None], error_1[None])
 
-    mine, shard_error = average(seconds, [own_piece] + got_pieces, [0] + across)
+    mine, shard_error = average(seconds)
 
     arrived = {0: mine}
     for step in back:
-        arrived[step] = send_chip(mine, step, nodes)
+        arrived[step] = send_chip(mine, step, nodes, crossed_back(step))
     order = [0] + back
     given = {}
     for step in order:

time: 38.4 us -> 34.1 us (0.89)
  starting transfers between devices: 19 us -> 14.2 us
  waiting for transfers between devices: 13.2 us -> 13.8 us
    ppermute x6 -> x3, starting transfers between devices: 8.23 us -> 3.55 us  [send_group(): lax.ppermute(values, 'group', [(i, target(i, step, groups)) for i in rang...]
    ppermute x6 -> x3, waiting for transfers between devices: 2.97 us -> 3.73 us  [send_group(): lax.ppermute(values, 'group', [(i, target(i, step, groups)) for i in rang...]
    ppermute x6, starting transfers between devices: 8.67 us -> 8.14 us  [send_chip(): return lax.ppermute(values, 'node', pairs)]
    ppermute x6, starting transfers between devices: 2.06 us -> 2.51 us  [swap_cores(): return lax.ppermute(values, 'node', [(i, i ^ 1) for i in range(nodes)])]
  transfers between devices with their start and end apart: 18 -> 15, of which waited for: 8 -> 8; matrix products, arithmetic and copies ran while one was open for 0% -> 0% of each run, Pallas kernels for 6% -> 7%
where the time goes in v3:
time: 34.1 us; the launch traced here: 33.9 us
  starting transfers between devices  14.2 us (42%)
  waiting for transfers between devices  13.8 us (40%)
  Pallas kernels  5.08 us (15%)
  between operations  0.8 us (2%)
    ppermute x6, waiting for transfers between devices, send_chip(): return lax.ppermute(values, 'node', pairs)  8.87 us
    ppermute x6, starting transfers between devices, send_chip(): return lax.ppermute(values, 'node', pairs)  8.14 us
    ppermute x3, waiting for transfers between devices, send_group(): lax.ppermute(values, 'group', [(i, target(i, step, groups)) for i in rang...  3.73 us
    ppermute x3, starting transfers between devices, send_group(): lax.ppermute(values, 'group', [(i, target(i, step, groups)) for i in rang...  3.55 us
    ppermute x6, starting transfers between devices, swap_cores(): return lax.ppermute(values, 'node', [(i, i ^ 1) for i in range(nodes)])  2.51 us
    pallas_call x2, Pallas kernels, update(): pl.pallas_call(functools.partial(update_kernel, steps, chips), out_shape=...  1.63 us
    pallas_call x1, Pallas kernels, head(): pl.pallas_call(functools.partial(head_kernel, order, joined), out_shape=[...  1.53 us
    ppermute x6, waiting for transfers between devices, swap_cores(): return lax.ppermute(values, 'node', [(i, i ^ 1) for i in range(nodes)])  1.19 us
  transfers between devices with their start and end apart: 15, of which 8 were waited for; matrix products, arithmetic and copies ran while one was open for 0% of the time, Pallas kernels for 7%

profile of v3, /device:TPU:0, one launch (start us, length us, event | category | flops | bytes accessed | tf_op | source)
XLA Modules:
  0.0 33.9 jit_solution(11514448395381842531)
XLA Ops:
  0.6 1.5 %shard_map.127 = (f32[16,1024]{1,0:T(8,128)S(1)}, f32[16,1024]{1,0:T(8,128)S(1)}, f32[16,1024]{1,0:T(8,128)S(1)}, f32[16,1024]{1,0:T(8,128)S(1)}, f32[16,1024]{1...) custom-call(bf16[1,1,128,1024]{3,2,1,0:T(8,128)(2,1)} %gradient.1, f32[128,1024]{1,0:T(8,128)} %momentum.1, ...), custom_call_target="tpu_custom_call" | custom-call | tf_op jit(solution)/shard_map/pallas_call | solution.py:130
  2.2 0.6 %collective-permute-start = (f32[3,16,1024]{2,1,0:T(8,128)S(1)}, f32[3,16,1024]{2,1,0:T(8,128)S(1)}, u32[]{:S(2)}, u32[]{:S(2)}) collective-permute-start(f32[3,16,1024]{2,1,0:T(8,128)S(1)} %get-tuple-element.29), channel_id=1, source_target_pairs={{0,4},{4,0},{8,12},{12,8},{16,20},{20,16},{24,28},{28,24},{1,5},{5... | collective-permute-start | bytes 589832 | tf_op jit(solution)/shard_map/ppermute | solution.py:48
  2.7 0.1 collective-permute-start.1
  2.8 1.2 %collective-permute-done.1 = f32[16,1024]{1,0:T(8,128)S(1)} collective-permute-done((f32[16,1024]{1,0:T(8,128)S(1)}, f32[16,1024]{1,0:T(8,128)S(1)}, u32[]{:S(2)}, u32[]{:S(2)}) %collective-permute-start.1) | collective-permute-done | bytes 65568 | tf_op jit(solution)/shard_map/ppermute | solution.py:48
  4.0 4.8 %collective-permute-start.2 = (f32[16,1024]{1,0:T(8,128)S(1)}, f32[16,1024]{1,0:T(8,128)S(1)}, u32[]{:S(2)}, u32[]{:S(2)}) collective-permute-start(f32[16,1024]{1,0:T(8,128)S(1)} %add.9), channel_id=1, source_target_pairs={{0,28},{4,24},{8,20},{12,16},{16,12},{20,8},{24,4},{28,0},{1,29},{... | collective-permute-start | bytes 196616 | tf_op jit(solution)/shard_map/ppermute | solution.py:58
  8.8 0.0 collective-permute-done
  8.8 0.0 copy-start.4
  8.8 0.1 collective-permute-start.3
  8.9 0.0 copy-start.2
  8.9 0.0 copy-start.3
  8.9 0.5 %collective-permute-start.4 = (f32[16,1024]{1,0:T(8,128)S(1)}, f32[16,1024]{1,0:T(8,128)S(1)}, u32[]{:S(2)}, u32[]{:S(2)}) collective-permute-start(f32[16,1024]{1,0:T(8,128)S(1)} %get-tuple-element.50), channel_id=1, source_target_pairs={{0,12},{4,8},{8,4},{12,0},{16,28},{20,24},{24,20},{28,16},{1,13},{... | collective-permute-start | bytes 196616 | tf_op jit(solution)/shard_map/ppermute | solution.py:58
  9.3 1.9 %collective-permute-done.2.refs_2_ = f32[16,1024]{1,0:T(8,128)S(1)} collective-permute-done((f32[16,1024]{1,0:T(8,128)S(1)}, f32[16,1024]{1,0:T(8,128)S(1)}, u32[]{:S(2)}, u32[]{:S(2)}) %collective-permute-start.2) | collective-permute-done | bytes 65568 | tf_op jit(solution)/shard_map/ppermute | solution.py:58
  11.3 3.2 %collective-permute-done.3.refs_3_ = f32[16,1024]{1,0:T(8,128)S(1)} collective-permute-done((f32[16,1024]{1,0:T(8,128)S(1)}, f32[16,1024]{1,0:T(8,128)S(1)}, u32[]{:S(2)}, u32[]{:S(2)}) %collective-permute-start.3) | collective-permute-done | bytes 65568 | tf_op jit(solution)/shard_map/ppermute | solution.py:58
  14.5 0.0 collective-permute-done.4.refs_4_
  14.5 0.0 copy-done.4
  14.5 0.0 copy-done.2
  14.5 0.0 copy-done.3
  14.6 0.0 copy-start.1
  14.6 0.2 shard_map.128
  14.8 0.0 copy-start
  14.8 2.5 %collective-permute-start.5 = (f32[16,1024]{1,0:T(8,128)S(1)}, f32[16,1024]{1,0:T(8,128)S(1)}, u32[]{:S(2)}, u32[]{:S(2)}) collective-permute-start(f32[16,1024]{1,0:T(8,128)S(1)} %get-tuple-element.34.refs_0_), channel_id=1, source_target_pairs={{0,3},{1,2},{2,1},{3,0},{4,7},{5,6},{6,5},{7,4},{8,11},{9,10},{10,... | collective-permute-start | bytes 196616 | tf_op jit(solution)/shard_map/ppermute | solution.py:62
  17.3 0.5 %collective-permute-start.6 = (f32[16,1024]{1,0:T(8,128)S(1)}, f32[16,1024]{1,0:T(8,128)S(1)}, u32[]{:S(2)}, u32[]{:S(2)}) collective-permute-start(f32[16,1024]{1,0:T(8,128)S(1)} %get-tuple-element.34.refs_0_), channel_id=1, source_target_pairs={{0,2},{1,3},{2,0},{3,1},{4,6},{5,7},{6,4},{7,5},{8,10},{9,11},{10,... | collective-permute-start | bytes 196616 | tf_op jit(solution)/shard_map/ppermute | solution.py:62
  17.8 0.5 %collective-permute-start.7 = (f32[16,1024]{1,0:T(8,128)S(1)}, f32[16,1024]{1,0:T(8,128)S(1)}, u32[]{:S(2)}, u32[]{:S(2)}) collective-permute-start(f32[16,1024]{1,0:T(8,128)S(1)} %get-tuple-element.34.refs_0_), channel_id=1, source_target_pairs={{0,1},{1,0},{2,3},{3,2},{4,5},{5,4},{6,7},{7,6},{8,9},{9,8},{10,11... | collective-permute-start | bytes 196616 | tf_op jit(solution)/shard_map/ppermute | solution.py:62
  18.3 1.7 %collective-permute-done.5.refs_1_ = f32[16,1024]{1,0:T(8,128)S(1)} collective-permute-done((f32[16,1024]{1,0:T(8,128)S(1)}, f32[16,1024]{1,0:T(8,128)S(1)}, u32[]{:S(2)}, u32[]{:S(2)}) %collective-permute-start.5) | collective-permute-done | bytes 65568 | tf_op jit(solution)/shard_map/ppermute | solution.py:62
  20.0 1.5 %collective-permute-done.6.refs_2_ = f32[16,1024]{1,0:T(8,128)S(1)} collective-permute-done((f32[16,1024]{1,0:T(8,128)S(1)}, f32[16,1024]{1,0:T(8,128)S(1)}, u32[]{:S(2)}, u32[]{:S(2)}) %collective-permute-start.6) | collective-permute-done | bytes 65568 | tf_op jit(solution)/shard_map/ppermute | solution.py:62
  21.6 0.5 %collective-permute-done.7.refs_3_ = f32[16,1024]{1,0:T(8,128)S(1)} collective-permute-done((f32[16,1024]{1,0:T(8,128)S(1)}, f32[16,1024]{1,0:T(8,128)S(1)}, u32[]{:S(2)}, u32[]{:S(2)}) %collective-permute-start.7) | collective-permute-done | bytes 65568 | tf_op jit(solution)/shard_map/ppermute | solution.py:62
  22.1 0.1 shard_map.129
  22.2 0.1 collective-permute-start.10
  22.3 1.3 %collective-permute-start.11 = (f32[16,1024]{1,0:T(8,128)S(1)}, f32[16,1024]{1,0:T(8,128)S(1)}, u32[]{:S(2)}, u32[]{:S(2)}) collective-permute-start(f32[16,1024]{1,0:T(8,128)S(1)} %get-tuple-element.35.mine), channel_id=1, source_target_pairs={{0,8},{4,12},{8,0},{12,4},{16,24},{20,28},{24,16},{28,20},{1,9},{5... | collective-permute-start | bytes 196616 | tf_op jit(solution)/shard_map/ppermute | solution.py:58
  23.6 1.5 %collective-permute-start.8 = (f32[16,1024]{1,0:T(8,128)S(1)}, f32[16,1024]{1,0:T(8,128)S(1)}, u32[]{:S(2)}, u32[]{:S(2)}) collective-permute-start(f32[16,1024]{1,0:T(8,128)S(1)} %get-tuple-element.35.mine), channel_id=1, source_target_pairs={{0,24},{4,28},{8,16},{12,20},{16,8},{20,12},{24,0},{28,4},{1,25},{... | collective-permute-start | bytes 196616 | tf_op jit(solution)/shard_map/ppermute | solution.py:58
  25.0 1.1 %collective-permute-start.14 = (f32[16,1024]{1,0:T(8,128)S(1)}, f32[16,1024]{1,0:T(8,128)S(1)}, u32[]{:S(2)}, u32[]{:S(2)}) collective-permute-start(f32[16,1024]{1,0:T(8,128)S(1)} %get-tuple-element.35.mine), channel_id=1, source_target_pairs={{0,4},{4,0},{8,12},{12,8},{16,20},{20,16},{24,28},{28,24},{1,5},{5... | collective-permute-start | bytes 196616 | tf_op jit(solution)/shard_map/ppermute | solution.py:48
  26.2 2.4 %collective-permute-done.10.refs_0_ = f32[16,1024]{1,0:T(8,128)S(1)} collective-permute-done((f32[16,1024]{1,0:T(8,128)S(1)}, f32[16,1024]{1,0:T(8,128)S(1)}, u32[]{:S(2)}, u32[]{:S(2)}) %collective-permute-start.10) | collective-permute-done | bytes 65568 | tf_op jit(solution)/shard_map/ppermute | solution.py:58
  28.6 0.0 collective-permute-start.12
  28.6 0.0 collective-permute-done.11.refs_1_
  28.6 0.5 %collective-permute-start.13 = (f32[16,1024]{1,0:T(8,128)S(1)}, f32[16,1024]{1,0:T(8,128)S(1)}, u32[]{:S(2)}, u32[]{:S(2)}) collective-permute-start(f32[16,1024]{1,0:T(8,128)S(1)} %collective-permute-done.11.refs_1_), channel_id=1, source_target_pairs={{0,4},{4,0},{8,12},{12,8},{16,20},{20,16},{24,28},{28,24},{1,5},{5... | collective-permute-start | bytes 196616 | tf_op jit(solution)/shard_map/ppermute | solution.py:48
  29.1 1.3 %collective-permute-done.8.refs_0_ = f32[16,1024]{1,0:T(8,128)S(1)} collective-permute-done((f32[16,1024]{1,0:T(8,128)S(1)}, f32[16,1024]{1,0:T(8,128)S(1)}, u32[]{:S(2)}, u32[]{:S(2)}) %collective-permute-start.8) | collective-permute-done | bytes 65568 | tf_op jit(solution)/shard_map/ppermute | solution.py:58
  30.4 0.2 collective-permute-start.9
  30.6 0.8 %shard_map.133 = (f32[1,1,128,1024]{3,2,1,0:T(8,128)}, f32[1,16,1024]{2,1,0:T(8,128)}, f32[1,16,1024]{2,1,0:T(8,128)}) custom-call(f32[1,1,128,1024]{3,2,1,0:T(8,128)S(1)} %bitcast.15, f32[1,16,1024]{2,1,0:T(8,128)S(1)} %bitcast.16, f32[1,16,1024]{2,1,0:T(8,128)S(1)} %bitcast.17), custom_call_target="tpu_custom_call" | custom-call | tf_op jit(solution)/shard_map/pallas_call | solution.py:185
  31.5 0.0 collective-permute-done.14.given
  31.5 0.0 copy-done.1
  31.5 0.0 copy-done
  31.5 0.8 %shard_map.130 = (f32[128,1024]{1,0:T(8,128)}, f32[128,1024]{1,0:T(8,128)}, f32[4,1024]{1,0:T(4,128)}) custom-call(f32[16,1024]{1,0:T(8,128)S(1)} %get-tuple-element.35.mine, f32[16,1024]{1,0:T(8,128)S(1)} %collective-permute-done.14.given, f32[128,1024]{1,0:T(8,128)S(1)} %copy-done, f32[128,1024]{1,0:T(8,128)S(1)} %copy-done.1, ...), custom_call_target="tpu_custom_call" | custom-call | tf_op jit(solution)/shard_map/pallas_call | solution.py:231
  32.3 0.0 collective-permute-done.12.refs_2_
  32.3 0.0 collective-permute-done.13.refs_3_
  32.3 0.9 %shard_map.131 = (f32[128,1024]{1,0:T(8,128)}, f32[128,1024]{1,0:T(8,128)}) custom-call(f32[16,1024]{1,0:T(8,128)S(1)} %collective-permute-done.10.refs_0_, f32[16,1024]{1,0:T(8,128)S(1)} %collective-permute-done.11.refs_1_, f32[16,1024]{1,0:T(8,128)S(1)} %collective-permute-done.12.refs_2_, ...), custom_call_target="tpu_custom_call", output_to_operand_aliasing={{0}: (6, {}), {1}: (7, {})} | custom-call | tf_op jit(solution)/shard_map/pallas_call | solution.py:272
  33.2 0.0 collective-permute-done.9.refs_1_
  33.2 0.8 %shard_map.132 = (f32[128,1024]{1,0:T(8,128)}, f32[128,1024]{1,0:T(8,128)}) custom-call(f32[16,1024]{1,0:T(8,128)S(1)} %collective-permute-done.8.refs_0_, f32[16,1024]{1,0:T(8,128)S(1)} %collective-permute-done.9.refs_1_, f32[128,1024]{1,0:T(8,128)S(1)} %copy-done, f32[128,1024]{1,0:T(8,128)S(1)} %copy-done.1, ...), custom_call_target="tpu_custom_call", output_to_operand_aliasing={{0}: (4, {}), {1}: (5, {})} | custom-call | tf_op jit(solution)/shard_map/pallas_call | solution.py:272
  (3 shorter events, 0.0 us)
Async XLA Ops:
  2.2 6.6 %collective-permute-start = (f32[3,16,1024]{2,1,0:T(8,128)S(1)}, f32[3,16,1024]{2,1,0:T(8,128)S(1)}, u32[]{:S(2)}, u32[]{:S(2)}) collective-permute-start(f32[3,16,1024]{2,1,0:T(8,128)S(1)} %get-tuple-element.29), channel_id=1, source_target_pairs={{0,4},{4,0},{8,12},{12,8},{16,20},{20,16},{24,28},{28,24},{1,5},{5... | collective-permute-start | bytes 589832 | tf_op jit(solution)/shard_map/ppermute | solution.py:48
  2.7 1.3 %collective-permute-start.1 = (f32[16,1024]{1,0:T(8,128)S(1)}, f32[16,1024]{1,0:T(8,128)S(1)}, u32[]{:S(2)}, u32[]{:S(2)}) collective-permute-start(f32[16,1024]{1,0:T(8,128)S(1)} %get-tuple-element.31), channel_id=1, source_target_pairs={{0,4},{4,0},{8,12},{12,8},{16,20},{20,16},{24,28},{28,24},{1,5},{5... | collective-permute-start | bytes 196616 | tf_op jit(solution)/shard_map/ppermute | solution.py:48
  4.0 7.3 %collective-permute-start.2 = (f32[16,1024]{1,0:T(8,128)S(1)}, f32[16,1024]{1,0:T(8,128)S(1)}, u32[]{:S(2)}, u32[]{:S(2)}) collective-permute-start(f32[16,1024]{1,0:T(8,128)S(1)} %add.9), channel_id=1, source_target_pairs={{0,28},{4,24},{8,20},{12,16},{16,12},{20,8},{24,4},{28,0},{1,29},{... | collective-permute-start | bytes 196616 | tf_op jit(solution)/shard_map/ppermute | solution.py:58
  8.8 5.8 %copy-start.4 = (f32[4,1024]{1,0:T(4,128)S(1)}, f32[4,1024]{1,0:T(4,128)}, u32[]{:S(2)}) copy-start(f32[4,1024]{1,0:T(4,128)} %refs_7_.1) | copy-start | bytes 49156
  8.8 5.7 %collective-permute-start.3 = (f32[16,1024]{1,0:T(8,128)S(1)}, f32[16,1024]{1,0:T(8,128)S(1)}, u32[]{:S(2)}, u32[]{:S(2)}) collective-permute-start(f32[16,1024]{1,0:T(8,128)S(1)} %get-tuple-element.51), channel_id=1, source_target_pairs={{0,20},{4,16},{8,28},{12,24},{16,4},{20,0},{24,12},{28,8},{1,21},{... | collective-permute-start | bytes 196616 | tf_op jit(solution)/shard_map/ppermute | solution.py:58
  8.9 5.7 %copy-start.2 = (f32[1,16,1024]{2,1,0:T(8,128)S(1)}, f32[1,16,1024]{2,1,0:T(8,128)}, u32[]{:S(2)}) copy-start(f32[1,16,1024]{2,1,0:T(8,128)} %param.13) | copy-start | bytes 196612
  8.9 5.7 %copy-start.3 = (f32[1,16,1024]{2,1,0:T(8,128)S(1)}, f32[1,16,1024]{2,1,0:T(8,128)}, u32[]{:S(2)}) copy-start(f32[1,16,1024]{2,1,0:T(8,128)} %param.14) | copy-start | bytes 196612
  8.9 5.6 %collective-permute-start.4 = (f32[16,1024]{1,0:T(8,128)S(1)}, f32[16,1024]{1,0:T(8,128)S(1)}, u32[]{:S(2)}, u32[]{:S(2)}) collective-permute-start(f32[16,1024]{1,0:T(8,128)S(1)} %get-tuple-element.50), channel_id=1, source_target_pairs={{0,12},{4,8},{8,4},{12,0},{16,28},{20,24},{24,20},{28,16},{1,13},{... | collective-permute-start | bytes 196616 | tf_op jit(solution)/shard_map/ppermute | solution.py:58
  14.6 16.9 %copy-start.1 = (f32[128,1024]{1,0:T(8,128)S(1)}, f32[128,1024]{1,0:T(8,128)}, u32[]{:S(2)}) copy-start(f32[128,1024]{1,0:T(8,128)} %refs_3_.1) | copy-start | bytes 1572868
  14.8 16.7 %copy-start = (f32[128,1024]{1,0:T(8,128)S(1)}, f32[128,1024]{1,0:T(8,128)}, u32[]{:S(2)}) copy-start(f32[128,1024]{1,0:T(8,128)} %refs_2_.1) | copy-start | bytes 1572868
  14.8 5.2 %collective-permute-start.5 = (f32[16,1024]{1,0:T(8,128)S(1)}, f32[16,1024]{1,0:T(8,128)S(1)}, u32[]{:S(2)}, u32[]{:S(2)}) collective-permute-start(f32[16,1024]{1,0:T(8,128)S(1)} %get-tuple-element.34.refs_0_), channel_id=1, source_target_pairs={{0,3},{1,2},{2,1},{3,0},{4,7},{5,6},{6,5},{7,4},{8,11},{9,10},{10,... | collective-permute-start | bytes 196616 | tf_op jit(solution)/shard_map/ppermute | solution.py:62
  17.3 4.3 %collective-permute-start.6 = (f32[16,1024]{1,0:T(8,128)S(1)}, f32[16,1024]{1,0:T(8,128)S(1)}, u32[]{:S(2)}, u32[]{:S(2)}) collective-permute-start(f32[16,1024]{1,0:T(8,128)S(1)} %get-tuple-element.34.refs_0_), channel_id=1, source_target_pairs={{0,2},{1,3},{2,0},{3,1},{4,6},{5,7},{6,4},{7,5},{8,10},{9,11},{10,... | collective-permute-start | bytes 196616 | tf_op jit(solution)/shard_map/ppermute | solution.py:62
  17.8 4.3 %collective-permute-start.7 = (f32[16,1024]{1,0:T(8,128)S(1)}, f32[16,1024]{1,0:T(8,128)S(1)}, u32[]{:S(2)}, u32[]{:S(2)}) collective-permute-start(f32[16,1024]{1,0:T(8,128)S(1)} %get-tuple-element.34.refs_0_), channel_id=1, source_target_pairs={{0,1},{1,0},{2,3},{3,2},{4,5},{5,4},{6,7},{7,6},{8,9},{9,8},{10,11... | collective-permute-start | bytes 196616 | tf_op jit(solution)/shard_map/ppermute | solution.py:62
  22.2 6.4 %collective-permute-start.10 = (f32[16,1024]{1,0:T(8,128)S(1)}, f32[16,1024]{1,0:T(8,128)S(1)}, u32[]{:S(2)}, u32[]{:S(2)}) collective-permute-start(f32[16,1024]{1,0:T(8,128)S(1)} %get-tuple-element.35.mine), channel_id=1, source_target_pairs={{0,20},{4,16},{8,28},{12,24},{16,4},{20,0},{24,12},{28,8},{1,21},{... | collective-permute-start | bytes 196616 | tf_op jit(solution)/shard_map/ppermute | solution.py:58
  22.3 6.3 %collective-permute-start.11 = (f32[16,1024]{1,0:T(8,128)S(1)}, f32[16,1024]{1,0:T(8,128)S(1)}, u32[]{:S(2)}, u32[]{:S(2)}) collective-permute-start(f32[16,1024]{1,0:T(8,128)S(1)} %get-tuple-element.35.mine), channel_id=1, source_target_pairs={{0,8},{4,12},{8,0},{12,4},{16,24},{20,28},{24,16},{28,20},{1,9},{5... | collective-permute-start | bytes 196616 | tf_op jit(solution)/shard_map/ppermute | solution.py:58
  23.6 6.8 %collective-permute-start.8 = (f32[16,1024]{1,0:T(8,128)S(1)}, f32[16,1024]{1,0:T(8,128)S(1)}, u32[]{:S(2)}, u32[]{:S(2)}) collective-permute-start(f32[16,1024]{1,0:T(8,128)S(1)} %get-tuple-element.35.mine), channel_id=1, source_target_pairs={{0,24},{4,28},{8,16},{12,20},{16,8},{20,12},{24,0},{28,4},{1,25},{... | collective-permute-start | bytes 196616 | tf_op jit(solution)/shard_map/ppermute | solution.py:58
  25.0 6.4 %collective-permute-start.14 = (f32[16,1024]{1,0:T(8,128)S(1)}, f32[16,1024]{1,0:T(8,128)S(1)}, u32[]{:S(2)}, u32[]{:S(2)}) collective-permute-start(f32[16,1024]{1,0:T(8,128)S(1)} %get-tuple-element.35.mine), channel_id=1, source_target_pairs={{0,4},{4,0},{8,12},{12,8},{16,20},{20,16},{24,28},{28,24},{1,5},{5... | collective-permute-start | bytes 196616 | tf_op jit(solution)/shard_map/ppermute | solution.py:48
  28.6 3.7 %collective-permute-start.12 = (f32[16,1024]{1,0:T(8,128)S(1)}, f32[16,1024]{1,0:T(8,128)S(1)}, u32[]{:S(2)}, u32[]{:S(2)}) collective-permute-start(f32[16,1024]{1,0:T(8,128)S(1)} %collective-permute-done.10.refs_0_), channel_id=1, source_target_pairs={{0,4},{4,0},{8,12},{12,8},{16,20},{20,16},{24,28},{28,24},{1,5},{5... | collective-permute-start | bytes 196616 | tf_op jit(solution)/shard_map/ppermute | solution.py:48
  28.6 3.7 %collective-permute-start.13 = (f32[16,1024]{1,0:T(8,128)S(1)}, f32[16,1024]{1,0:T(8,128)S(1)}, u32[]{:S(2)}, u32[]{:S(2)}) collective-permute-start(f32[16,1024]{1,0:T(8,128)S(1)} %collective-permute-done.11.refs_1_), channel_id=1, source_target_pairs={{0,4},{4,0},{8,12},{12,8},{16,20},{20,16},{24,28},{28,24},{1,5},{5... | collective-permute-start | bytes 196616 | tf_op jit(solution)/shard_map/ppermute | solution.py:48
  30.4 2.8 %collective-permute-start.9 = (f32[16,1024]{1,0:T(8,128)S(1)}, f32[16,1024]{1,0:T(8,128)S(1)}, u32[]{:S(2)}, u32[]{:S(2)}) collective-permute-start(f32[16,1024]{1,0:T(8,128)S(1)} %collective-permute-done.8.refs_0_), channel_id=1, source_target_pairs={{0,4},{4,0},{8,12},{12,8},{16,20},{20,16},{24,28},{28,24},{1,5},{5... | collective-permute-start | bytes 196616 | tf_op jit(solution)/shard_map/ppermute | solution.py:48
